TPU v7x, 128 devices: a whole 4x4x4 slice. The times are simulated.
128 devices in a mesh: row: 8 (over x, core), col: 16 (over z, y).
Axes of the slice: x: 4, y: 4, z: 4, core: 2. Of those that a mesh axis runs over, the one named last changes fastest.
Arguments:
- coords: float32 [3, 2097152], P(None, ('row', 'col')), may hold values from 0 to 6
- vectors: bfloat16 [64, 2097152], P(None, ('row', 'col')), may hold values from -0.59765625 to 0.59765625
- basis: bfloat16 [32, 2097152], P(None, ('row', 'col')), may hold values from -1.5 to 1.5
- transfer: float32 [32, 262144], P(None, ('row', 'col')), may hold values from -0.3 to 0.3
- leaf_skeleton: float32 [3, 262144], P(None, ('row', 'col')), may hold values from 0 to 6
- device_skeleton: float32 [3, 4096], P(None, ('row', 'col')), may hold values from 0 to 6
- near_pairs: int32 [2, 49152], P(None, ('row', 'col')), may hold values from 0 to 8191, as said below
- far_leaves: int32 [8192, 8], P(('row', 'col')), may hold values from 0 to 8191, as said below
- far_devices: int32 [128, 16], P(('row', 'col')), may hold values from 0 to 127
Outputs:
- product: float32 [64, 2097152], P(None, ('row', 'col'))
Inputs may be any that keep to these rules, and one draw needn't show every extreme that they name: `near_pairs`: device k of the row x col grid (k = row index * 16 + col index) holds near blocks k * 6 * 64 to (k + 1) * 6 * 64 - 1 and leaves k * 64 to (k + 1) * 64 - 1; the target and the source leaf of each of its near blocks lie on device k or on a device beside it in the grid, diagonals included. `far_leaves`: the coupling partners of a leaf lie on that leaf's device or on a device beside it in the row x col grid, diagonals included.
All inputs are finite; a program needn't handle non-finite values.
Results may differ from a plain program's by a relative error of at most 0.004.
Values may be sent and summed in bfloat16 or wider, within the bound.
A program may use at most 256 MiB of HBM per device.

v0:
```python
import math

import jax
import jax.numpy as jnp
from jax import lax
from jax.sharding import PartitionSpec as P

HIGH = lax.Precision.HIGHEST


def with_halo(array, sides, width):
    for axis, dim in sides:
        devices, length = (lax.axis_size(axis), array.shape[dim])
        up = [(i, (i + 1) % devices) for i in range(devices - 1)]
        down = [(j, i) for i, j in up]
        last = lax.slice_in_dim(array, length - width, length, axis=dim)
        initial = lax.slice_in_dim(array, 0, width, axis=dim)
        before = lax.ppermute(last, axis, up)
        after = lax.ppermute(initial, axis, down)
        array = jnp.concatenate([before, array, after], axis=dim)
    return array


def from_behind(block, axis, distance):
    devices = range(lax.axis_size(axis))
    route = [(i - distance, i) for i in devices if i - distance in devices]
    return lax.ppermute(block, axis, route)


def turned_gather(arrays, axis, dims):
    turned = [jnp.moveaxis(a, dim, 0) for a, dim in zip(arrays, dims)]
    both = jnp.concatenate([t.reshape(len(t), -1) for t in turned], axis=1)
    result, at, outs = (lax.all_gather(both, axis, axis=0, tiled=True), 0, [])
    for t, dim in zip(turned, dims):
        share = result[:, at : at + t[0].size].reshape(-1, *t.shape[1:])
        outs.append(jnp.moveaxis(share, 0, dim))
        at += t[0].size
    return tuple(outs)


def kernel_block(left, right):
    total = None
    for dimension in range(3):
        gap = left[..., dimension, :, None] - right[..., dimension, None, :]
        total = gap * gap if total is None else total + gap * gap
    return jnp.exp(-0.5 * total)


def upsweep(vector_rows, basis_rows):
    return jnp.einsum(
        "nvil,nril->nvir", vector_rows, basis_rows, preferred_element_type=jnp.float32
    ).astype(jnp.bfloat16)


def shards(
    coords,
    vectors,
    basis,
    transfer,
    leaf_skeleton,
    device_skeleton,
    near_pairs,
    far_leaves,
    far_devices,
):
    col_count = lax.axis_size("col")
    row_here = lax.axis_index("row")
    col_here = lax.axis_index("col")
    rank_size = basis.shape[0]
    vec_count = vectors.shape[0]
    leaves = transfer.shape[1] // rank_size
    leaf_width = coords.shape[1] // leaves
    block_group = math.gcd(near_pairs.shape[1], 32)

    def hood_of(global_leaf):
        owner_dev = global_leaf // leaves
        row_offset = owner_dev // col_count - row_here + 1
        col_offset = owner_dev % col_count - col_here + 1
        return (row_offset * 3 + col_offset, global_leaf % leaves)

    points_pad, skeleton_pad = (
        with_halo(coords[None, None], (("row", 0), ("col", 1)), 1),
        with_halo(leaf_skeleton[None, None], (("row", 0), ("col", 1)), 1),
    )
    vectors_pad, basis_pad = (
        with_halo(vectors[None, None], (("row", 0), ("col", 1)), 1),
        with_halo(basis[None, None], (("row", 0), ("col", 1)), 1),
    )
    coeff_pad = upsweep(
        vectors_pad.reshape(9, vec_count, leaves, leaf_width),
        basis_pad.reshape(9, rank_size, leaves, leaf_width),
    )
    coeff_own = coeff_pad[4]
    coords_pool = points_pad.reshape(9, 3, leaves, leaf_width)
    vectors_pool = vectors_pad.reshape(9, vec_count, leaves, leaf_width)
    tgt_hood, tgt_leaf = hood_of(near_pairs[0].reshape(-1, block_group))
    src_hood, src_leaf = hood_of(near_pairs[1].reshape(-1, block_group))

    def near_step(buffer, item):
        t_hood, t_leaf, s_hood, s_leaf = item
        tgt_points = coords_pool[t_hood, :, t_leaf, :]
        src_points = coords_pool[s_hood, :, s_leaf, :]
        block = kernel_block(tgt_points, src_points).astype(jnp.bfloat16)
        src_vectors = vectors_pool[s_hood, :, s_leaf, :]
        partial_value = jnp.einsum(
            "bvs,bts->bvt", src_vectors, block, preferred_element_type=jnp.float32
        )
        return (buffer.at[t_hood, :, t_leaf, :].add(partial_value), None)

    start = jnp.zeros((9, vec_count, leaves, leaf_width), jnp.float32)
    buffer, _ = lax.scan(near_step, start, (tgt_hood, tgt_leaf, src_hood, src_leaf))
    buffer = buffer.reshape(3, 3, vec_count, leaves * leaf_width)
    near_field = buffer[1, 1]
    for row_step in range(3):
        for col_step in range(3):
            if row_step != 1 or col_step != 1:
                offset = (row_step - 1) * col_count + (col_step - 1)
                near_field = near_field + from_behind(
                    buffer[row_step, col_step].astype(jnp.bfloat16), ("row", "col"), offset
                ).astype(jnp.float32)
    far_hood, far_leaf = hood_of(far_leaves)
    picked_coeff = coeff_pad[far_hood, :, far_leaf, :].astype(jnp.float32)
    skeleton_pool = skeleton_pad.reshape(9, 3, leaves, rank_size)
    picked_skel = skeleton_pool[far_hood, :, far_leaf, :]
    own_skel = jnp.transpose(leaf_skeleton.reshape(3, leaves, rank_size), (1, 0, 2))
    coupling = kernel_block(picked_skel, own_skel[:, None])
    leaf_far = jnp.einsum("ifvs,ifst->ivt", picked_coeff, coupling, precision=HIGH)
    transfer_mats = transfer.reshape(rank_size, leaves, rank_size)
    device_coeff = jnp.einsum(
        "vir,ris->vs", coeff_own.astype(jnp.float32), transfer_mats, precision=HIGH
    )
    all_coeffs, all_skeleton = turned_gather(
        (device_coeff, device_skeleton), ("row", "col"), (1, 1)
    )
    chosen = far_devices[0]
    top_coeffs = all_coeffs.reshape(vec_count, -1, rank_size)[:, chosen, :]
    top_skel = jnp.transpose(all_skeleton.reshape(3, -1, rank_size)[:, chosen, :], (1, 0, 2))
    coupling_top = kernel_block(top_skel, device_skeleton[None])
    device_far = jnp.einsum("vfs,fst->vt", top_coeffs, coupling_top, precision=HIGH)
    field = leaf_far + jnp.einsum("vs,ris->ivr", device_far, transfer_mats, precision=HIGH)
    field = field.astype(jnp.bfloat16)
    far_part = jnp.einsum(
        "ivr,ril->vil",
        field,
        basis.reshape(rank_size, leaves, leaf_width),
        preferred_element_type=jnp.float32,
    )
    return near_field + far_part.reshape(vec_count, leaves * leaf_width)


def solution(mesh):
    in_specs = (
        P(None, ("row", "col")),
        P(None, ("row", "col")),
        P(None, ("row", "col")),
        P(None, ("row", "col")),
        P(None, ("row", "col")),
        P(None, ("row", "col")),
        P(None, ("row", "col")),
        P(("row", "col"), None),
        P(("row", "col"), None),
    )
    out_specs = P(None, ("row", "col"))
    return jax.shard_map(shards, mesh=mesh, in_specs=in_specs, out_specs=out_specs, check_vma=False)
```

profile of v0, /device:TPU:35, one launch (start us, length us, event | category | flops | bytes accessed | tf_op | source)
XLA Modules:
  0.0 949.8 jit_solution(7944079981632862380)
XLA Ops:
  7.8 3.7 collective-permute-start.4
  20.9 3.6 collective-permute-start
  34.6 4.3 collective-permute-start.19
  40.9 11.7 %collective-permute-done.1 = bf16[1,1,64,16384]{3,2,1,0:T(8,128)(2,1)S(1)} collective-permute-done((bf16[1,1,64,16384]{3,2,1,0:T(8,128)(2,1)}, bf16[1,1,64,16384]{3,2,1,0:T(8,128)(2,1)S(1)}, u32[]{:S(2)}, u32[]{:S(2)}) %collective-permute-start.1) | collective-permute-done | bytes 2097184 | tf_op jit(solution)/shard_map/ppermute | solution.py:19
  56.9 4.2 collective-permute-start.3
  63.8 5.5 collective-permute-start.7
  72.3 180.6 %collective-permute-done.7 = f32[3,1,3,16384]{3,1,2,0:T(1,128)} collective-permute-done((f32[3,1,3,16384]{3,1,2,0:T(1,128)}, f32[3,1,3,16384]{3,1,2,0:T(1,128)}, u32[]{:S(2)}, u32[]{:S(2)}) %collective-permute-start.7) | collective-permute-done | bytes 589856 | tf_op jit(solution)/shard_map/ppermute | solution.py:19
  257.3 13.5 %collective-permute-done.6 = f32[3,1,3,16384]{3,1,2,0:T(1,128)S(1)} collective-permute-done((f32[3,1,3,16384]{3,1,2,0:T(1,128)}, f32[3,1,3,16384]{3,1,2,0:T(1,128)S(1)}, u32[]{:S(2)}, u32[]{:S(2)}) %collective-permute-start.6) | collective-permute-done | bytes 589856 | tf_op jit(solution)/shard_map/ppermute | solution.py:18
  270.9 4.7 collective-permute-start.21
  283.8 7.8 pad_maximum_fusion.1
  291.6 10.5 %copy.76 = bf16[36,8,64,256]{3,2,1,0:T(8,128)(2,1)} copy(bf16[36,8,64,256]{3,1,2,0:T(8,128)(2,1)} %bitcast.197) | data formatting | bytes 18874368
  302.2 7.1 pad_maximum_fusion
  309.3 4.5 copy.75
  313.9 12.0 %copy.53 = bf16[9,64,64,256]{3,1,2,0:T(8,128)(2,1)} copy(bf16[9,64,64,256]{3,2,1,0:T(8,128)(2,1)S(1)} %bitcast.194) | data formatting | bytes 37748736 | tf_op jit(solution)/shard_map/while | solution.py:111
  325.9 12.6 %broadcast_in_dim.26 = f32[9,64,64,256]{3,1,2,0:T(8,128)} broadcast(f32[]{:T(128)} %constant.129.clone.1), dimensions={} | broadcast | bytes 37748740 | tf_op jit(solution)/shard_map/broadcast_in_dim | solution.py:110
  338.5 303.9 %while.10 = (s32[]{:T(128)}, f32[9,64,64,256]{3,1,2,0:T(8,128)}, s32[12,32]{1,0:T(8,128)S(1)}, s32[12,32]{1,0:T(8,128)S(1)}, s32[12,32]{1,0:T(8,128)S(1)}, /*ind...) while((s32[]{:T(128)}, f32[9,64,64,256]{3,1,2,0:T(8,128)}, ...), condition=%wide.region_2.3_spmd, body=%wide.region_0.2_spmd.sunk | while | flops 289932096 | bytes 12912617 | solution.py:111
  343.4 7.0 gather_fusion
  350.4 7.0 fusion.137
  357.4 6.5 scatter_fusion
  368.8 7.0 gather_fusion
  375.8 7.0 fusion.137
  382.7 6.4 scatter_fusion
  394.1 7.0 gather_fusion
  401.1 7.0 fusion.137
  408.1 6.4 scatter_fusion
  419.4 7.0 gather_fusion
  426.4 7.0 fusion.137
  433.4 6.4 scatter_fusion
  444.7 7.0 gather_fusion
  451.7 7.0 fusion.137
  458.7 6.4 scatter_fusion
  470.0 7.0 gather_fusion
  477.0 7.0 fusion.137
  484.0 6.4 scatter_fusion
  495.3 7.0 gather_fusion
  502.3 7.0 fusion.137
  509.2 6.4 scatter_fusion
  520.6 7.0 gather_fusion
  527.6 7.0 fusion.137
  534.5 6.4 scatter_fusion
  545.9 7.0 gather_fusion
  552.9 7.0 fusion.137
  559.8 6.4 scatter_fusion
  571.2 7.0 gather_fusion
  578.2 7.0 fusion.137
  585.2 6.4 scatter_fusion
  596.5 7.0 gather_fusion
  603.5 7.0 fusion.137
  610.5 6.5 scatter_fusion
  621.9 7.0 gather_fusion
  628.9 7.0 fusion.137
  635.9 6.5 scatter_fusion
  642.4 35.3 %copy.55 = f32[9,64,64,256]{3,2,1,0:T(8,128)} copy(f32[9,64,64,256]{3,1,2,0:T(8,128)} %get-tuple-element.47) | data formatting | bytes 75497472 | tf_op jit(solution)/shard_map/while | solution.py:111
  677.6 40.3 %reshape.193 = f32[3,3,64,16384]{3,2,1,0:T(8,128)} reshape(f32[9,64,64,256]{3,2,1,0:T(8,128)} %copy.55) | data formatting | bytes 75497472 | tf_op jit(solution)/shard_map/reshape | solution.py:112
  718.0 13.1 %convert.10 = bf16[3,3,64,16384]{3,2,1,0:T(8,128)(2,1)S(1)} convert(f32[3,3,64,16384]{3,2,1,0:T(8,128)} %reshape.193) | non-fusion elementwise | flops 9437184 | bytes 56623104 | tf_op jit(solution)/shard_map/convert.7
  731.0 5.9 slice_bitcast_fusion.8
  746.4 28.9 %convert_bitcast_fusion = bf16[9,64,64,32]{1,3,2,0:T(8,128)(2,1)} fusion(bf16[9,32,64,256]{3,2,1,0:T(8,128)(2,1)} %bitcast.200, bf16[9,64,64,256]{3,2,1,0:T(8,128)(2,1)} %bitcast.195), kind=kOutput, calls=%fused_computation.59 | convolution fusion | flops 605159424 | bytes 30670848 | tf_op jit(solution)/shard_map/nvil,nril->nvir/dot_general | solution.py:50
  779.5 5.2 collective-permute-start.23
  789.2 4.1 collective-permute-done.22
  801.0 4.2 collective-permute-start.12
  814.1 8.4 gather_fusion.3
  822.4 12.3 %fusion.47 = f32[64,64,32]{1,2,0:T(8,128)S(1)} fusion(bf16[64,8,64,32]{2,3,1,0:T(8,128)(2,1)} %bitcast.199, f32[64,32]{1,0:T(8,128)S(1)} %copy-done.12, f32[64,8,32]{2,1,0:T(8,128)S(1)} %bitcast.222, f32[64,32]{1,0:T(8,128)S(1)} %copy-done.13, f32[64,8,32]{2,1,0:T(8,128)S(1)} %bitcast.221, f32[64,32]{1,0:T(8,128)S(1)} %copy-done.11, ...), kind=kOutput, calls=%fused_computation.88 | convolution fusion | flops 407371776 | bytes 2842624 | tf_op jit(solution)/shard_map/ifvs,ifst->ivt/dot_general | solution.py:127
  834.8 83.6 %all-gather.2.cloned.1.call-done = f32[4096,67]{1,0:T(8,128)} async-done(((f32[32,67]{1,0:T(8,128)}), f32[4096,67]{1,0:T(8,128)}) %all-gather.2.cloned.1.call-update) | async-done | bytes 1097744 | tf_op jit(solution)/shard_map/all_gather | solution.py:33
  932.3 10.2 %fusion.37 = f32[64,16384]{1,0:T(8,128)} fusion(f32[64,16384]{1,0:T(8,128)S(1)} %bitcast.198, f32[3,3,64,16384]{3,2,1,0:T(8,128)} %reshape.193, bf16[64,16384]{1,0:T(8,128)(2,1)} %collective-permute-done.15, bf16[64,16384]{1,0:T(8,128)(2,1)} %collective-permute-done.14, bf16[64,16384]{1,0:T(8,128)(2,1)} %collective-permute-done.13, ...), kind=kLoop, calls=%fused_computation.69 | loop fusion | flops 17825792 | bytes 29360128 | tf_op jit(solution)/shard_map/add | solution.py:148
  (249 shorter events, 151.9 us)
Async XLA Ops:
  6.5 47.0 %copy-start.4 = (bf16[64,16384]{1,0:T(8,128)(2,1)S(1)}, bf16[64,16384]{1,0:T(8,128)(2,1)}, u32[]{:S(2)}) copy-start(bf16[64,16384]{1,0:T(8,128)(2,1)} %param.12) | copy-start | bytes 6291460
  6.5 911.8 %all-gather.2.cloned.1.call-start = ((), (), s32[]{:S(2)}) async-start(), calls=%async_computation | async-start | bytes 2113536 | tf_op jit(solution)/shard_map/all_gather | solution.py:33
  7.8 13.1 %collective-permute-start.4 = (f32[1,1,3,16384]{3,1,2,0:T(1,128)S(1)}, f32[1,1,3,16384]{3,1,2,0:T(1,128)S(1)}, u32[]{:S(2)}, u32[]{:S(2)}) collective-permute-start(f32[1,1,3,16384]{3,1,2,0:T(1,128)S(1)} %broadcast_in_dim.28), channel_id=1, source_target_pairs={{0,16},{16,32},{32,48},{48,64},{64,80},{80,96},{96,112},{1,17},{17... | collective-permute-start | bytes 589832 | tf_op jit(solution)/shard_map/ppermute | solution.py:18
  11.5 51.6 %collective-permute-start.5 = (f32[1,1,3,16384]{3,1,2,0:T(1,128)S(1)}, f32[1,1,3,16384]{3,1,2,0:T(1,128)S(1)}, u32[]{:S(2)}, u32[]{:S(2)}) collective-permute-start(f32[1,1,3,16384]{3,1,2,0:T(1,128)S(1)} %broadcast_in_dim.28), channel_id=1, source_target_pairs={{16,0},{32,16},{48,32},{64,48},{80,64},{96,80},{112,96},{17,1},{33... | collective-permute-start | bytes 589832 | tf_op jit(solution)/shard_map/ppermute | solution.py:19
  13.4 16.6 %collective-permute-start.17 = (bf16[1,1,32,16384]{3,2,1,0:T(8,128)(2,1)}, bf16[1,1,32,16384]{3,2,1,0:T(8,128)(2,1)S(1)}, u32[]{:S(2)}, u32[]{:S(2)}) collective-permute-start(bf16[1,1,32,16384]{3,2,1,0:T(8,128)(2,1)} %bitcast.201), channel_id=1, source_target_pairs={{16,0},{32,16},{48,32},{64,48},{80,64},{96,80},{112,96},{17,1},{33... | collective-permute-start | bytes 3145736 | tf_op jit(solution)/shard_map/ppermute | solution.py:19
  15.9 15.1 %collective-permute-start.16 = (bf16[1,1,32,16384]{3,2,1,0:T(8,128)(2,1)}, bf16[1,1,32,16384]{3,2,1,0:T(8,128)(2,1)S(1)}, u32[]{:S(2)}, u32[]{:S(2)}) collective-permute-start(bf16[1,1,32,16384]{3,2,1,0:T(8,128)(2,1)} %bitcast.202), channel_id=1, source_target_pairs={{0,16},{16,32},{32,48},{48,64},{64,80},{80,96},{96,112},{1,17},{17... | collective-permute-start | bytes 3145736 | tf_op jit(solution)/shard_map/ppermute | solution.py:18
  19.0 33.6 %collective-permute-start.1 = (bf16[1,1,64,16384]{3,2,1,0:T(8,128)(2,1)}, bf16[1,1,64,16384]{3,2,1,0:T(8,128)(2,1)S(1)}, u32[]{:S(2)}, u32[]{:S(2)}) collective-permute-start(bf16[1,1,64,16384]{3,2,1,0:T(8,128)(2,1)} %bitcast.206), channel_id=1, source_target_pairs={{16,0},{32,16},{48,32},{64,48},{80,64},{96,80},{112,96},{17,1},{33... | collective-permute-start | bytes 6291464 | tf_op jit(solution)/shard_map/ppermute | solution.py:19
  20.9 32.6 %collective-permute-start = (bf16[1,1,64,16384]{3,2,1,0:T(8,128)(2,1)}, bf16[1,1,64,16384]{3,2,1,0:T(8,128)(2,1)S(1)}, u32[]{:S(2)}, u32[]{:S(2)}) collective-permute-start(bf16[1,1,64,16384]{3,2,1,0:T(8,128)(2,1)} %bitcast.207), channel_id=1, source_target_pairs={{0,16},{16,32},{32,48},{48,64},{64,80},{80,96},{96,112},{1,17},{17... | collective-permute-start | bytes 6291464 | tf_op jit(solution)/shard_map/ppermute | solution.py:18
  31.0 25.9 %copy-start.7 = (bf16[1,1,32,16384]{3,2,1,0:T(8,128)(2,1)}, bf16[1,1,32,16384]{3,2,1,0:T(8,128)(2,1)S(1)}, u32[]{:S(2)}) copy-start(bf16[1,1,32,16384]{3,2,1,0:T(8,128)(2,1)S(1)} %collective-permute-done.16) | copy-start | bytes 3145732
  34.6 34.6 %copy-start.18 = (s32[2,384]{1,0:T(2,128)S(1)}, s32[2,384]{1,0:T(2,128)}, u32[]{:S(2)}) copy-start(s32[2,384]{1,0:T(2,128)} %param.17) | copy-start | bytes 9220
  34.6 34.8 %copy-start.15 = (f32[3,32]{1,0:T(4,128)S(1)}, f32[3,32]{1,0:T(4,128)}, u32[]{:S(2)}) copy-start(f32[3,32]{1,0:T(4,128)} %param.16) | copy-start | bytes 1156
  34.6 36.4 %copy-start.9 = (f32[32,2048]{1,0:T(8,128)S(1)}, f32[32,2048]{1,0:T(8,128)}, u32[]{:S(2)}) copy-start(f32[32,2048]{1,0:T(8,128)} %param.14) | copy-start | bytes 786436
  34.6 221.4 %copy-start.17 = (s32[64,8]{0,1:T(8,128)S(1)}, s32[64,8]{0,1:T(8,128)}, u32[]{:S(2)}) copy-start(s32[64,8]{0,1:T(8,128)} %param.18) | copy-start | bytes 6148
  34.6 246.6 %collective-permute-start.19 = (bf16[3,1,32,16384]{3,2,1,0:T(8,128)(2,1)}, bf16[3,1,32,16384]{3,2,1,0:T(8,128)(2,1)}, u32[]{:S(2)}, u32[]{:S(2)}) collective-permute-start(bf16[3,1,32,16384]{3,2,1,0:T(8,128)(2,1)} %pad_maximum_fusion.3), channel_id=1, source_target_pairs={{1,0},{2,1},{3,2},{4,3},{5,4},{6,5},{7,6},{8,7},{9,8},{10,9},{11,1... | collective-permute-start | bytes 9437192 | tf_op jit(solution)/shard_map/ppermute | solution.py:19
  39.0 244.9 %collective-permute-start.18 = (bf16[3,1,32,16384]{3,2,1,0:T(8,128)(2,1)}, bf16[3,1,32,16384]{3,2,1,0:T(8,128)(2,1)}, u32[]{:S(2)}, u32[]{:S(2)}) collective-permute-start(bf16[3,1,32,16384]{3,2,1,0:T(8,128)(2,1)} %pad_maximum_fusion.3), channel_id=1, source_target_pairs={{0,1},{1,2},{2,3},{3,4},{4,5},{5,6},{6,7},{7,8},{8,9},{9,10},{10,1... | collective-permute-start | bytes 9437192 | tf_op jit(solution)/shard_map/ppermute | solution.py:18
  52.6 4.3 copy-start.5
  53.5 3.5 copy-start.6
  56.9 245.2 %collective-permute-start.3 = (bf16[3,1,64,16384]{3,2,1,0:T(8,128)(2,1)}, bf16[3,1,64,16384]{3,2,1,0:T(8,128)(2,1)}, u32[]{:S(2)}, u32[]{:S(2)}) collective-permute-start(bf16[3,1,64,16384]{3,2,1,0:T(8,128)(2,1)} %pad_maximum_fusion.2), channel_id=1, source_target_pairs={{1,0},{2,1},{3,2},{4,3},{5,4},{6,5},{7,6},{8,7},{9,8},{10,9},{11,1... | collective-permute-start | bytes 18874376 | tf_op jit(solution)/shard_map/ppermute | solution.py:19
  61.1 241.0 %collective-permute-start.2 = (bf16[3,1,64,16384]{3,2,1,0:T(8,128)(2,1)}, bf16[3,1,64,16384]{3,2,1,0:T(8,128)(2,1)}, u32[]{:S(2)}, u32[]{:S(2)}) collective-permute-start(bf16[3,1,64,16384]{3,2,1,0:T(8,128)(2,1)} %pad_maximum_fusion.2), channel_id=1, source_target_pairs={{0,1},{1,2},{2,3},{3,4},{4,5},{5,6},{6,7},{7,8},{8,9},{9,10},{10,1... | collective-permute-start | bytes 18874376 | tf_op jit(solution)/shard_map/ppermute | solution.py:18
  63.8 189.1 %collective-permute-start.7 = (f32[3,1,3,16384]{3,1,2,0:T(1,128)}, f32[3,1,3,16384]{3,1,2,0:T(1,128)}, u32[]{:S(2)}, u32[]{:S(2)}) collective-permute-start(f32[3,1,3,16384]{3,1,2,0:T(1,128)} %constant_dynamic-update-slice_fusion), channel_id=1, source_target_pairs={{1,0},{2,1},{3,2},{4,3},{5,4},{6,5},{7,6},{8,7},{9,8},{10,9},{11,1... | collective-permute-start | bytes 1769480 | tf_op jit(solution)/shard_map/ppermute | solution.py:19
  252.9 18.0 %collective-permute-start.6 = (f32[3,1,3,16384]{3,1,2,0:T(1,128)}, f32[3,1,3,16384]{3,1,2,0:T(1,128)S(1)}, u32[]{:S(2)}, u32[]{:S(2)}) collective-permute-start(f32[3,1,3,16384]{3,1,2,0:T(1,128)} %constant_dynamic-update-slice_fusion), channel_id=1, source_target_pairs={{0,1},{1,2},{2,3},{3,4},{4,5},{5,6},{6,7},{7,8},{8,9},{9,10},{10,1... | collective-permute-start | bytes 1769480 | tf_op jit(solution)/shard_map/ppermute | solution.py:18
  270.9 12.9 %copy-start.2 = (bf16[32,16384]{1,0:T(8,128)(2,1)S(1)}, bf16[32,16384]{1,0:T(8,128)(2,1)}, u32[]{:S(2)}) copy-start(bf16[32,16384]{1,0:T(8,128)(2,1)} %param.13) | copy-start | bytes 3145732
  270.9 13.0 %copy-start.8 = (bf16[1,1,32,16384]{3,2,1,0:T(8,128)(2,1)S(1)}, bf16[1,1,32,16384]{3,2,1,0:T(8,128)(2,1)}, u32[]{:S(2)}) copy-start(bf16[1,1,32,16384]{3,2,1,0:T(8,128)(2,1)} %copy-done.7) | copy-start | bytes 3145732
  270.9 507.8 %collective-permute-start.21 = (f32[1,1,3,2048]{3,2,1,0:T(4,128)}, f32[1,1,3,2048]{3,2,1,0:T(4,128)}, u32[]{:S(2)}, u32[]{:S(2)}) collective-permute-start(f32[1,1,3,2048]{3,2,1,0:T(4,128)} %bitcast.21), channel_id=1, source_target_pairs={{16,0},{32,16},{48,32},{64,48},{80,64},{96,80},{112,96},{17,1},{33... | collective-permute-start | bytes 73736 | tf_op jit(solution)/shard_map/ppermute | solution.py:19
  281.2 497.5 %collective-permute-start.20 = (f32[1,1,3,2048]{3,2,1,0:T(4,128)}, f32[1,1,3,2048]{3,2,1,0:T(4,128)}, u32[]{:S(2)}, u32[]{:S(2)}) collective-permute-start(f32[1,1,3,2048]{3,2,1,0:T(4,128)} %bitcast.21), channel_id=1, source_target_pairs={{0,16},{16,32},{32,48},{48,64},{64,80},{80,96},{96,112},{1,17},{17... | collective-permute-start | bytes 73736 | tf_op jit(solution)/shard_map/ppermute | solution.py:18
  313.8 12.0 %copy-start = (bf16[72,8,64,256]{3,2,1,0:T(8,128)(2,1)}, bf16[72,8,64,256]{3,2,1,0:T(8,128)(2,1)S(1)}, u32[]{:S(2)}) copy-start(bf16[72,8,64,256]{3,2,1,0:T(8,128)(2,1)S(1)} %copy.75) | copy-start | bytes 56623108
  737.0 68.2 %collective-permute-start.8 = (bf16[64,16384]{1,0:T(8,128)(2,1)}, bf16[64,16384]{1,0:T(8,128)(2,1)}, u32[]{:S(2)}, u32[]{:S(2)}) collective-permute-start(bf16[64,16384]{1,0:T(8,128)(2,1)} %get-tuple-element.115), channel_id=1, source_target_pairs={{17,0},{18,1},{19,2},{20,3},{21,4},{22,5},{23,6},{24,7},{25,8},{26... | collective-permute-start | bytes 6291464 | tf_op jit(solution)/shard_map/ppermute | solution.py:27
  740.4 68.1 %collective-permute-start.15 = (bf16[64,16384]{1,0:T(8,128)(2,1)}, bf16[64,16384]{1,0:T(8,128)(2,1)}, u32[]{:S(2)}, u32[]{:S(2)}) collective-permute-start(bf16[64,16384]{1,0:T(8,128)(2,1)} %get-tuple-element.116), channel_id=1, source_target_pairs={{0,17},{1,18},{2,19},{3,20},{4,21},{5,22},{6,23},{7,24},{8,25},{9,... | collective-permute-start | bytes 6291464 | tf_op jit(solution)/shard_map/ppermute | solution.py:27
  743.4 67.0 %collective-permute-start.14 = (bf16[64,16384]{1,0:T(8,128)(2,1)}, bf16[64,16384]{1,0:T(8,128)(2,1)}, u32[]{:S(2)}, u32[]{:S(2)}) collective-permute-start(bf16[64,16384]{1,0:T(8,128)(2,1)} %get-tuple-element.117), channel_id=1, source_target_pairs={{0,16},{1,17},{2,18},{3,19},{4,20},{5,21},{6,22},{7,23},{8,24},{9,... | collective-permute-start | bytes 6291464 | tf_op jit(solution)/shard_map/ppermute | solution.py:27
  746.4 29.0 %copy-start.1 = (f32[32,64,32]{2,1,0:T(8,128)S(1)}, f32[32,64,32]{2,1,0:T(8,128)}, u32[]{:S(2)}) copy-start(f32[32,64,32]{2,1,0:T(8,128)} %reshape.197) | copy-start | bytes 786436
  746.4 31.3 %copy-start.10 = (f32[3,32]{0,1:T(8,128)S(1)}, f32[3,32]{0,1:T(8,128)}, u32[]{:S(2)}) copy-start(f32[3,32]{0,1:T(8,128)} %copy.61) | copy-start | bytes 1156
  746.4 32.0 %copy-start.16 = (f32[3,32]{1,0:T(4,128)S(1)}, f32[3,32]{1,0:T(4,128)}, u32[]{:S(2)}) copy-start(f32[3,32]{1,0:T(4,128)} %param.16) | copy-start | bytes 1156
  746.4 32.1 %copy-start.19 = (s32[1,16]{1,0:T(1,128)S(1)}, s32[1,16]{1,0:T(1,128)}, u32[]{:S(2)}) copy-start(s32[1,16]{1,0:T(1,128)} %param.19) | copy-start | bytes 196
  746.4 32.1 %copy-start.14 = (s32[64,8]{0,1:T(8,128)S(1)}, s32[64,8]{0,1:T(8,128)}, u32[]{:S(2)}) copy-start(s32[64,8]{0,1:T(8,128)} %fusion.107) | copy-start | bytes 6148
  779.5 9.6 %collective-permute-start.23 = (f32[3,1,3,2048]{3,2,1,0:T(4,128)S(1)}, f32[3,1,3,2048]{3,2,1,0:T(4,128)S(1)}, u32[]{:S(2)}, u32[]{:S(2)}) collective-permute-start(f32[3,1,3,2048]{3,2,1,0:T(4,128)S(1)} %pad_maximum_fusion.6), channel_id=1, source_target_pairs={{1,0},{2,1},{3,2},{4,3},{5,4},{6,5},{7,6},{8,7},{9,8},{10,9},{11,1... | collective-permute-start | bytes 221192 | tf_op jit(solution)/shard_map/ppermute | solution.py:19
  784.7 8.6 collective-permute-start.22
  797.6 134.6 %collective-permute-start.13 = (bf16[64,16384]{1,0:T(8,128)(2,1)}, bf16[64,16384]{1,0:T(8,128)(2,1)}, u32[]{:S(2)}, u32[]{:S(2)}) collective-permute-start(bf16[64,16384]{1,0:T(8,128)(2,1)} %get-tuple-element.118), channel_id=1, source_target_pairs={{0,15},{1,16},{2,17},{3,18},{4,19},{5,20},{6,21},{7,22},{8,23},{9,... | collective-permute-start | bytes 6291464 | tf_op jit(solution)/shard_map/ppermute | solution.py:27
  801.0 131.2 %collective-permute-start.12 = (bf16[64,16384]{1,0:T(8,128)(2,1)}, bf16[64,16384]{1,0:T(8,128)(2,1)}, u32[]{:S(2)}, u32[]{:S(2)}) collective-permute-start(bf16[64,16384]{1,0:T(8,128)(2,1)} %get-tuple-element.119), channel_id=1, source_target_pairs={{0,1},{1,2},{2,3},{3,4},{4,5},{5,6},{6,7},{7,8},{8,9},{9,10},{10,1... | collective-permute-start | bytes 6291464 | tf_op jit(solution)/shard_map/ppermute | solution.py:27
  805.2 127.0 %collective-permute-start.11 = (bf16[64,16384]{1,0:T(8,128)(2,1)}, bf16[64,16384]{1,0:T(8,128)(2,1)}, u32[]{:S(2)}, u32[]{:S(2)}) collective-permute-start(bf16[64,16384]{1,0:T(8,128)(2,1)} %get-tuple-element.120), channel_id=1, source_target_pairs={{1,0},{2,1},{3,2},{4,3},{5,4},{6,5},{7,6},{8,7},{9,8},{10,9},{11,1... | collective-permute-start | bytes 6291464 | tf_op jit(solution)/shard_map/ppermute | solution.py:27
  808.5 123.8 %collective-permute-start.10 = (bf16[64,16384]{1,0:T(8,128)(2,1)}, bf16[64,16384]{1,0:T(8,128)(2,1)}, u32[]{:S(2)}, u32[]{:S(2)}) collective-permute-start(bf16[64,16384]{1,0:T(8,128)(2,1)} %get-tuple-element.121), channel_id=1, source_target_pairs={{15,0},{16,1},{17,2},{18,3},{19,4},{20,5},{21,6},{22,7},{23,8},{24... | collective-permute-start | bytes 6291464 | tf_op jit(solution)/shard_map/ppermute | solution.py:27
  810.4 121.8 %collective-permute-start.9 = (bf16[64,16384]{1,0:T(8,128)(2,1)}, bf16[64,16384]{1,0:T(8,128)(2,1)}, u32[]{:S(2)}, u32[]{:S(2)}) collective-permute-start(bf16[64,16384]{1,0:T(8,128)(2,1)} %get-tuple-element.122), channel_id=1, source_target_pairs={{16,0},{17,1},{18,2},{19,3},{20,4},{21,5},{22,6},{23,7},{24,8},{25... | collective-permute-start | bytes 6291464 | tf_op jit(solution)/shard_map/ppermute | solution.py:27
  814.0 8.4 copy-start.11
  814.0 8.4 copy-start.12
  814.0 8.4 copy-start.13
  921.9 9.2 copy-start.3
Sparse Core Ops, SparseCore 0:
  778.6 139.7 all-gather.1
where the time goes:
time: 964 us; the launch traced here: 950 us
  waiting for transfers between devices  301 us (31%)
  local copies, waits for them, and re-layouts  298 us (31%)
  matrix products  130 us (13%)
  other arithmetic  128 us (13%)
  starting transfers between devices  77.3 us (8%)
  between operations  14.5 us (2%)
    ppermute x8, waiting for transfers between devices, with_halo(): after = lax.ppermute(initial, axis, down)  198 us
    gather x12, local copies, waits for them, and re-layouts, near_step(): src_vectors = vectors_pool[s_hood, :, s_leaf, :]  83.9 us
    all_gather x1, waiting for transfers between devices, turned_gather(): result, at, outs = (lax.all_gather(both, axis, axis=0, tiled=True), 0, [])  83.6 us
    dot_general x12, matrix products, near_step(): jnp.einsum('bvs,bts->bvt', src_vectors, block, preferred_element_type=jnp...  83.5 us
    scatter-add x12, other arithmetic, near_step(): return (buffer.at[t_hood, :, t_leaf, :].add(partial_value), None)  77.1 us
    while x2, local copies, waits for them, and re-layouts, shards(): lax.scan(near_step, start, (tgt_hood, tgt_leaf, src_hood, src_leaf))  47.3 us
    reshape x1, local copies, waits for them, and re-layouts, shards(): buffer = buffer.reshape(3, 3, vec_count, leaves * leaf_width)  40.3 us
    ppermute x8, starting transfers between devices, with_halo(): after = lax.ppermute(initial, axis, down)  30.3 us
  transfers between devices with their start and end apart: 25, of which 9 were waited for; matrix products, arithmetic and copies ran while one was open for 57% of the time, Pallas kernels for 0%

commit v1 on v0

v1 whole, which is shorter than its diff:
```python
import functools
import math

import jax
import jax.numpy as jnp
from jax import lax
from jax.experimental import pallas as pl
from jax.experimental.pallas import tpu as pltpu
from jax.sharding import PartitionSpec as P

HIGH = lax.Precision.HIGHEST
F32 = jnp.float32
BF16 = jnp.bfloat16
MESH = pl.DeviceIdType.MESH
SCALE = math.sqrt(math.log2(math.e))
MIDDLE = 3.0
CHUNK = 16


def point_features(points):
    scaled = (points - MIDDLE) * SCALE
    high = lax.reduce_precision(scaled, 8, 7)
    low = lax.reduce_precision(scaled - high, 8, 7)
    whole = high + low
    norm = -0.5 * (whole[0:1] ** 2 + whole[1:2] ** 2 + whole[2:3] ** 2)
    norm_high = lax.reduce_precision(norm, 8, 7)
    return jnp.concatenate([high, norm_high, low, norm - norm_high], axis=0).astype(BF16)


def kernel_block(left, right):
    total = None
    for dimension in range(3):
        gap = left[..., dimension, :, None] - right[..., dimension, None, :]
        total = gap * gap if total is None else total + gap * gap
    return jnp.exp(-0.5 * total)


def remote(src, dst, send, recv, device):
    return pltpu.make_async_remote_copy(
        src_ref=src, dst_ref=dst, send_sem=send, recv_sem=recv, device_id=device, device_id_type=MESH
    )


def halo_kernel(
    rows, cols, vec, geo, coeff, share,
    vec_pool, geo_pool, coeff_pool, every,
    row_share, send, recv, row_send, row_recv, col_send, col_recv, local,
):
    row, col = lax.axis_index("row"), lax.axis_index("col")
    barrier = pltpu.get_barrier_semaphore()
    for d in range(1, rows):
        pl.semaphore_signal(barrier, inc=1, device_id=(lax.rem(row + d, rows), col), device_id_type=MESH)
    for d in range(1, cols):
        pl.semaphore_signal(barrier, inc=1, device_id=(row, lax.rem(col + d, cols)), device_id_type=MESH)
    pl.semaphore_wait(barrier, rows + cols - 2)

    chunks = vec.shape[0] // CHUNK
    items = chunks + 2
    order = [0, chunks, chunks + 1] + list(range(1, chunks))

    def own(item):
        if item < chunks:
            return vec.at[pl.ds(item * CHUNK, CHUNK)]
        return geo if item == chunks else coeff

    def slot(hood, item):
        if item < chunks:
            return vec_pool.at[hood, pl.ds(item * CHUNK, CHUNK)]
        return (geo_pool if item == chunks else coeff_pool).at[hood]

    def copy(src, hood, item, device):
        return remote(src, slot(hood, item), send.at[hood, item], recv.at[hood, item], device)

    has_up, has_down = row > 0, row < rows - 1
    has_left, has_right = col > 0, col < cols - 1
    up, down, left, right = (row - 1, col), (row + 1, col), (row, col - 1), (row, col + 1)

    row_copies = []
    for d in range(1, rows):
        c = remote(share, row_share.at[row], row_send.at[d], row_recv.at[d], (lax.rem(row + d, rows), col))
        c.start()
        row_copies.append(c)
    keep_share = pltpu.make_async_copy(share, row_share.at[row], local.at[0])
    keep_share.start()
    keeps = [
        pltpu.make_async_copy(vec, vec_pool.at[4], local.at[1]),
        pltpu.make_async_copy(geo, geo_pool.at[4], local.at[2]),
        pltpu.make_async_copy(coeff, coeff_pool.at[4], local.at[3]),
    ]
    for k in keeps:
        k.start()

    direct = [(has_right, right, 3), (has_left, left, 5), (has_down, down, 1), (has_up, up, 7)]
    for item in order:
        for has, device, hood in direct:
            @pl.when(has)
            def _(device=device, hood=hood, item=item):
                copy(own(item), hood, item, device).start()

    keep_share.wait()
    for c in row_copies:
        c.wait_recv()
    col_copies = []
    for d in range(1, cols):
        c = remote(row_share, every.at[col], col_send.at[d], col_recv.at[d], (row, lax.rem(col + d, cols)))
        c.start()
        col_copies.append(c)
    keep_row = pltpu.make_async_copy(row_share, every.at[col], local.at[0])
    keep_row.start()

    passed = [(3, has_left, 0, 6), (5, has_right, 2, 8)]
    for item in order:
        for hood, has, to_down, to_up in passed:
            @pl.when(has)
            def _(hood=hood, item=item, to_down=to_down, to_up=to_up):
                copy(own(item), hood, item, down).wait_recv()

                @pl.when(has_down)
                def _():
                    copy(slot(hood, item), to_down, item, down).start()

                @pl.when(has_up)
                def _():
                    copy(slot(hood, item), to_up, item, up).start()

    keep_row.wait()
    for k in keeps:
        k.wait()
    for c in col_copies:
        c.wait_recv()
    for item in order:
        for has, hood in [
            (has_up, 1), (has_down, 7),
            (has_up & has_left, 0), (has_up & has_right, 2),
            (has_down & has_left, 6), (has_down & has_right, 8),
        ]:
            @pl.when(has)
            def _(hood=hood, item=item):
                copy(own(item), hood, item, down).wait_recv()
    for item in order:
        for has, hood in [
            (has_right, 3), (has_left, 5), (has_down, 1), (has_up, 7),
            (has_down & has_left, 0), (has_up & has_left, 6),
            (has_down & has_right, 2), (has_up & has_right, 8),
        ]:
            @pl.when(has)
            def _(hood=hood, item=item):
                copy(own(item), hood, item, down).wait_send()
    for c in row_copies + col_copies:
        c.wait_send()


def exchange(rows, cols, vec, geo, coeff, share):
    chunks = vec.shape[0] // CHUNK
    vmem = pl.BlockSpec(memory_space=pltpu.VMEM)
    hbm = pl.BlockSpec(memory_space=pl.ANY)
    pool = lambda a: jax.ShapeDtypeStruct((9, *a.shape), a.dtype)
    dma = pltpu.SemaphoreType.DMA
    return pl.pallas_call(
        functools.partial(halo_kernel, rows, cols),
        out_shape=(pool(vec), pool(geo), pool(coeff), jax.ShapeDtypeStruct((cols, rows, *share.shape), F32)),
        in_specs=[vmem] * 4,
        out_specs=(hbm, hbm, hbm, vmem),
        scratch_shapes=[
            pltpu.VMEM((rows, *share.shape), F32),
            dma((9, chunks + 2)), dma((9, chunks + 2)),
            dma((rows,)), dma((rows,)), dma((cols,)), dma((cols,)), dma((4,)),
        ],
        compiler_params=pltpu.CompilerParams(
            collective_id=0, has_side_effects=True, vmem_limit_bytes=24 * 2**20
        ),
        name="halo",
    )(vec, geo, coeff, share)


GROUP = 8
RING = 32
STAGES = 4


def near_kernel(
    blocks, leaves, index, vec_pool, geo_pool,
    partial, mine, feats, vbuf, acc, stage, touched, vsem, gsem, ssem,
):
    width = vbuf.shape[2]
    count = 9 * leaves
    share = stage.shape[1]
    geo_copy = pltpu.make_async_copy(geo_pool, feats, gsem.at[0])
    geo_copy.start()

    def fetch(p, slot):
        hood, leaf = index[2, p], index[3, p]
        return pltpu.make_async_copy(
            vec_pool.at[hood, :, pl.ds(pl.multiple_of(leaf * width, width), width)], vbuf.at[slot], vsem.at[slot]
        )

    for p in range(RING):
        fetch(p, p).start()

    @pl.loop(0, count)
    def _(i):
        touched[i] = 0

    geo_copy.wait()
    row_id = lax.broadcasted_iota(jnp.int32, (8, width), 0)
    unit = lax.rem(row_id, 4) == 3

    def features(hood, leaf):
        return feats[hood, :, pl.ds(pl.multiple_of(leaf * width, width), width)].astype(F32)

    def power(p):
        tgt = features(index[0, p], index[1, p])
        src = features(index[2, p], index[3, p])
        turned = jnp.concatenate([tgt[4:8], tgt[0:4]], axis=0)
        left = jnp.concatenate([src, jnp.where(unit, 1.0, src)], axis=0).astype(BF16)
        right = jnp.concatenate(
            [
                jnp.where(unit, 1.0, jnp.where(row_id < 4, tgt, turned)),
                jnp.where(row_id < 3, turned, tgt),
            ],
            axis=0,
        ).astype(BF16)
        return lax.dot_general(left, right, (((0,), (0,)), ((), ())), preferred_element_type=F32)

    @pl.loop(0, blocks // GROUP)
    def _(step):
        first = step * GROUP
        at = lax.rem(first, RING)
        for k in range(GROUP):
            fetch(first + k, at + k).wait()
        ahead = power(first)
        for k in range(GROUP):
            now = ahead
            if k + 1 < GROUP:
                ahead = power(first + k + 1)
            part = jnp.dot(vbuf[at + k], jnp.exp2(now).astype(BF16), preferred_element_type=F32)
            place = index[0, first + k] * leaves + index[1, first + k]
            seen = touched[place]
            touched[place] = 1
            acc[place] = jnp.where(seen > 0, acc[place], 0.0) + part

        @pl.when(first + RING < blocks)
        def _():
            for k in range(GROUP):
                fetch(first + RING + k, at + k).start()

    def settle(place):
        @pl.when(touched[place] == 0)
        def _():
            acc[place] = jnp.zeros(acc.shape[1:], F32)

    @pl.loop(0, leaves)
    def _(leaf):
        settle(4 * leaves + leaf)

    put_mine = pltpu.make_async_copy(acc.at[pl.ds(4 * leaves, leaves)], mine, gsem.at[0])
    put_mine.start()

    def put(hood, part):
        return pltpu.make_async_copy(
            stage.at[lax.rem(part, STAGES)], partial.at[hood, pl.ds(part * share, share)],
            ssem.at[lax.rem(part, STAGES)],
        )

    parts = leaves // share
    for hood in [h for h in range(9) if h != 4]:
        @pl.loop(0, parts)
        def _(part, hood=hood):
            if hood == 0:
                @pl.when(part >= STAGES)
                def _():
                    put(hood, part).wait()
            else:
                put(hood, part).wait()

            @pl.loop(0, share)
            def _(k):
                place = hood * leaves + part * share + k
                slot = lax.rem(part, STAGES)

                @pl.when(touched[place] > 0)
                def _():
                    stage[slot, k] = acc[place].astype(BF16)

                @pl.when(touched[place] == 0)
                def _():
                    stage[slot, k] = jnp.zeros(stage.shape[2:], BF16)

            put(hood, part).start()

    for slot in range(STAGES):
        put(0, slot).wait()
    put_mine.wait()


def near_blocks(index, vec_pool, geo_pool, leaves, width):
    blocks = index.shape[1]
    vecs = vec_pool.shape[1]
    share = leaves // STAGES
    hbm = pl.BlockSpec(memory_space=pl.ANY)
    dma = pltpu.SemaphoreType.DMA
    return pl.pallas_call(
        functools.partial(near_kernel, blocks, leaves),
        out_shape=(
            jax.ShapeDtypeStruct((9, leaves, vecs, width), BF16),
            jax.ShapeDtypeStruct((leaves, vecs, width), F32),
        ),
        in_specs=[pl.BlockSpec(memory_space=pltpu.SMEM), hbm, hbm],
        out_specs=(hbm, hbm),
        scratch_shapes=[
            pltpu.VMEM(geo_pool.shape, BF16),
            pltpu.VMEM((RING, vecs, width), BF16),
            pltpu.VMEM((9 * leaves, vecs, width), F32),
            pltpu.VMEM((STAGES, share, vecs, width), BF16),
            pltpu.SMEM((9 * leaves,), jnp.int32),
            dma((RING,)), dma((1,)), dma((STAGES,)),
        ],
        compiler_params=pltpu.CompilerParams(vmem_limit_bytes=58 * 2**20),
        name="near",
    )(index, vec_pool, geo_pool)


def return_kernel(
    rows, cols, chunks, partial, base, out,
    from_rows, sums, from_cols, row_send, row_recv, col_send, col_recv, local,
):
    row, col = lax.axis_index("row"), lax.axis_index("col")
    has_row = (row > 0, row < rows - 1)
    has_col = (col > 0, col < cols - 1)
    leaves, vecs, width = base.shape
    share = leaves // chunks
    loads = [
        pltpu.make_async_copy(partial.at[3], sums.at[0], local.at[0]),
        pltpu.make_async_copy(partial.at[5], sums.at[1], local.at[1]),
    ]
    for c in loads:
        c.start()
    barrier = pltpu.get_barrier_semaphore()
    row_dev = ((row - 1, col), (row + 1, col))
    col_dev = ((row, col - 1), (row, col + 1))
    peers = 0
    for has, dev in zip(has_row + has_col, row_dev + col_dev):
        peers = peers + has.astype(jnp.int32)

        @pl.when(has)
        def _(dev=dev):
            pl.semaphore_signal(barrier, inc=1, device_id=dev, device_id_type=MESH)
    pl.semaphore_wait(barrier, peers)

    def some(c):
        return pl.ds(c * share, share)

    def row_copy(side, place, c):
        hood = (0 if side == 0 else 6) + (0, 2, 1)[place]
        return remote(
            partial.at[hood, some(c)], from_rows.at[1 - side, place, some(c)],
            row_send.at[side, place, c], row_recv.at[1 - side, place, c], row_dev[side],
        )

    def col_copy(side, c):
        return remote(
            sums.at[side, some(c)], from_cols.at[1 - side, some(c)],
            col_send.at[side, c], col_recv.at[1 - side, c], col_dev[side],
        )

    wanted = has_col + (True,)
    plan = [(place, c) for c in range(chunks) for place in (0, 1)] + [(2, c) for c in range(chunks)]
    for place, c in plan:
        for side in (0, 1):
            @pl.when(has_row[side] & wanted[place])
            def _(side=side, place=place, c=c):
                row_copy(side, place, c).start()

    def fill(ref):
        @pl.loop(0, leaves)
        def _(i):
            ref[i] = jnp.zeros((vecs, width), BF16)

    for side in (0, 1):
        @pl.when(jnp.logical_not(has_row[side]))
        def _(side=side):
            for place in range(3):
                fill(from_rows.at[side, place])

        @pl.when(jnp.logical_not(has_col[side]))
        def _(side=side):
            fill(from_cols.at[side])

    for c in loads:
        c.wait()

    for c in range(chunks):
        for place in (0, 1):
            @pl.when(has_col[place])
            def _(place=place, c=c):
                for side in (0, 1):
                    @pl.when(has_row[side])
                    def _(side=side):
                        row_copy(1 - side, place, c).wait_recv()

                @pl.loop(c * share, (c + 1) * share)
                def _(i):
                    total = (
                        sums[place, i].astype(F32)
                        + from_rows[0, place, i].astype(F32)
                        + from_rows[1, place, i].astype(F32)
                    )
                    sums[place, i] = total.astype(BF16)

                col_copy(place, c).start()

    for c in range(chunks):
        for side in (0, 1):
            @pl.when(has_row[side])
            def _(side=side, c=c):
                row_copy(1 - side, 2, c).wait_recv()

            @pl.when(has_col[side])
            def _(side=side, c=c):
                col_copy(1 - side, c).wait_recv()

        @pl.loop(c * share, (c + 1) * share)
        def _(i):
            out[:, pl.ds(pl.multiple_of(i * width, width), width)] = (
                base[i]
                + from_rows[0, 2, i].astype(F32)
                + from_rows[1, 2, i].astype(F32)
                + from_cols[0, i].astype(F32)
                + from_cols[1, i].astype(F32)
            )

    for place, c in plan:
        for side in (0, 1):
            @pl.when(has_row[side] & wanted[place])
            def _(side=side, place=place, c=c):
                row_copy(side, place, c).wait_send()
    for c in range(chunks):
        for side in (0, 1):
            @pl.when(has_col[side])
            def _(side=side, c=c):
                col_copy(side, c).wait_send()


def give_back(rows, cols, partial, base):
    leaves, vecs, width = base.shape
    chunks = math.gcd(leaves, 4)
    vmem = pl.BlockSpec(memory_space=pltpu.VMEM)
    dma = pltpu.SemaphoreType.DMA
    return pl.pallas_call(
        functools.partial(return_kernel, rows, cols, chunks),
        out_shape=jax.ShapeDtypeStruct((vecs, leaves * width), F32),
        in_specs=[pl.BlockSpec(memory_space=pl.ANY), vmem],
        out_specs=vmem,
        scratch_shapes=[
            pltpu.VMEM((2, 3, leaves, vecs, width), BF16),
            pltpu.VMEM((2, leaves, vecs, width), BF16),
            pltpu.VMEM((2, leaves, vecs, width), BF16),
            dma((2, 3, chunks)), dma((2, 3, chunks)), dma((2, chunks)), dma((2, chunks)), dma((2,)),
        ],
        compiler_params=pltpu.CompilerParams(
            collective_id=1, has_side_effects=True, vmem_limit_bytes=48 * 2**20
        ),
        name="give_back",
    )(partial, base)


def shards(
    coords, vectors, basis, transfer, leaf_skeleton, device_skeleton, near_pairs, far_leaves, far_devices
):
    row_count, col_count = lax.axis_size("row"), lax.axis_size("col")
    row_here, col_here = lax.axis_index("row"), lax.axis_index("col")
    rank_size, vec_count = basis.shape[0], vectors.shape[0]
    leaves = transfer.shape[1] // rank_size
    leaf_width = coords.shape[1] // leaves
    points = coords.shape[1]

    def hood_of(global_leaf):
        owner = global_leaf // leaves
        hood = (owner // col_count - row_here + 1) * 3 + (owner % col_count - col_here + 1)
        return hood, global_leaf % leaves

    geo = point_features(jnp.concatenate([coords, leaf_skeleton], axis=1))
    coeff = jnp.einsum(
        "vil,ril->irv",
        vectors.reshape(vec_count, leaves, leaf_width),
        basis.reshape(rank_size, leaves, leaf_width),
        preferred_element_type=F32,
    ).astype(BF16)
    transfer_mats = transfer.reshape(rank_size, leaves, rank_size)
    device_coeff = jnp.einsum("irv,ris->vs", coeff.astype(F32), transfer_mats, precision=HIGH)
    paired = coeff.reshape(leaves // 2, 2, rank_size, vec_count)
    paired = jnp.transpose(paired, (0, 2, 1, 3)).reshape(leaves // 2 * rank_size, 2 * vec_count)
    flat = jnp.concatenate([device_coeff.reshape(-1), device_skeleton.reshape(-1)])
    flat = jnp.pad(flat, (0, -flat.size % 1024)).reshape(-1, 128)

    vec_pool, geo_pool, coeff_pool, every = exchange(row_count, col_count, vectors, geo, paired, flat)

    t_hood, t_leaf = hood_of(near_pairs[0])
    s_hood, s_leaf = hood_of(near_pairs[1])
    index = jnp.stack([t_hood, t_leaf, s_hood, s_leaf])
    partial, mine = near_blocks(index, vec_pool, geo_pool, leaves, leaf_width)

    far_hood, far_leaf = hood_of(far_leaves)
    skel = geo_pool[:, :, points:].astype(F32)
    skel = (skel[:, 0:3] + skel[:, 4:7]).reshape(9, 3, leaves, rank_size)
    picked_skel = skel[far_hood, :, far_leaf, :]
    own_skel = jnp.transpose(skel[4], (1, 0, 2))
    total = None
    for k in range(3):
        gap = picked_skel[..., k, :, None] - own_skel[:, None, k, None, :]
        total = gap * gap if total is None else total + gap * gap
    coupling = jnp.exp2(-0.5 * total)
    coeff_all = coeff_pool.reshape(9, leaves // 2, rank_size, 2, vec_count)
    picked_coeff = coeff_all[far_hood, far_leaf // 2, :, far_leaf % 2, :].astype(F32)
    leaf_far = jnp.einsum("ifsv,ifst->ivt", picked_coeff, coupling, precision=HIGH)

    chosen = far_devices[0]
    picked = every[chosen % col_count, chosen // col_count].reshape(chosen.shape[0], -1)
    size = vec_count * rank_size
    top_coeffs = picked[:, :size].reshape(-1, vec_count, rank_size)
    top_skel = picked[:, size : size + 3 * rank_size].reshape(-1, 3, rank_size)
    coupling_top = kernel_block(top_skel, device_skeleton[None])
    device_far = jnp.einsum("fvs,fst->vt", top_coeffs, coupling_top, precision=HIGH)
    field = leaf_far + jnp.einsum("vs,ris->ivr", device_far, transfer_mats, precision=HIGH)
    far_part = jnp.einsum(
        "ivr,ril->ivl",
        field.astype(BF16),
        basis.reshape(rank_size, leaves, leaf_width),
        preferred_element_type=F32,
    )
    base = mine + far_part
    return give_back(row_count, col_count, partial, base)


def solution(mesh):
    wide = P(None, ("row", "col"))
    tall = P(("row", "col"), None)
    return jax.shard_map(
        shards, mesh=mesh, in_specs=(wide,) * 7 + (tall,) * 2, out_specs=wide, check_vma=False
    )
```

time: 964 us -> 329 us (0.34); the launches traced: 950 us -> 329 us
  waiting for transfers between devices: 301 us -> 0 us
  Pallas kernels: 0 us -> 245 us
  local copies, waits for them, and re-layouts: 298 us -> 55.6 us
  other arithmetic: 128 us -> 7.06 us
  matrix products: 130 us -> 20.8 us
  starting transfers between devices: 77.3 us -> 0 us
  between operations: 14.5 us -> 0.33 us
    pallas_call x0 -> x3, Pallas kernels: none -> 245 us  [the longest x1 96 us: exchange(): pl.pallas_call(functools.partial(halo_kernel, rows, cols), out_shape=(poo...]
    ppermute x24 -> x0, waiting for transfers between devices: 217 us -> none  [the longest x8 198 us: with_halo(): after = lax.ppermute(initial, axis, down)]
    gather x40 -> x3, local copies, waits for them, and re-layouts: 155 us -> 15.2 us  [the longest x1 6.8 us: shards(): coeff_all[far_hood, far_leaf // 2, :, far_leaf % 2, :].astype(F32)]
    dot_general x17 -> x5, matrix products: 128 us -> 19.3 us  [the longest x1 9.77 us: shards(): jnp.einsum('ifsv,ifst->ivt', picked_coeff, coupling, precision=HIGH)]
    all_gather x1 -> x0, waiting for transfers between devices: 83.6 us -> none  [turned_gather(): result, at, outs = (lax.all_gather(both, axis, axis=0, tiled=True), 0, [])]
    ppermute x24 -> x0, starting transfers between devices: 77.3 us -> none  [the longest x8 30.3 us: with_halo(): after = lax.ppermute(initial, axis, down)]
    scatter-add x12 -> x0, other arithmetic: 77.1 us -> none  [near_step(): return (buffer.at[t_hood, :, t_leaf, :].add(partial_value), None)]
    while x74 -> x0, local copies, waits for them, and re-layouts: 47.6 us -> none  [the longest x2 47.3 us: shards(): lax.scan(near_step, start, (tgt_hood, tgt_leaf, src_hood, src_leaf))]
  transfers between devices with their start and end apart: 25 -> 0, of which waited for: 9 -> 0; matrix products, arithmetic and copies ran while one was open for 57% -> 0% of each run, Pallas kernels for 0% -> 0%
where the time goes in v1:
time: 329 us
  Pallas kernels  245 us (74%)
  local copies, waits for them, and re-layouts  55.6 us (17%)
  matrix products  20.8 us (6%)
  other arithmetic  7.06 us (2%)
    pallas_call x1, Pallas kernels, exchange(): pl.pallas_call(functools.partial(halo_kernel, rows, cols), out_shape=(poo...  96 us
    pallas_call x1, Pallas kernels, near_blocks(): pl.pallas_call(functools.partial(near_kernel, blocks, leaves), out_shape=...  74.9 us
    pallas_call x1, Pallas kernels, give_back(): pl.pallas_call(functools.partial(return_kernel, rows, cols, chunks), out_...  74 us
    unnamed x30, local copies, waits for them, and re-layouts  12.8 us
    reshape x2, local copies, waits for them, and re-layouts, shards(): coeff_all = coeff_pool.reshape(9, leaves // 2, rank_size, 2, vec_count)  9.91 us
    dot_general x1, matrix products, shards(): jnp.einsum('ifsv,ifst->ivt', picked_coeff, coupling, precision=HIGH)  9.77 us
    exp2 x1, local copies, waits for them, and re-layouts, shards(): coupling = jnp.exp2(-0.5 * total)  9.37 us
    gather x1, local copies, waits for them, and re-layouts, shards(): coeff_all[far_hood, far_leaf // 2, :, far_leaf % 2, :].astype(F32)  6.8 us

profile of v1, /device:TPU:35, one launch (start us, length us, event | category | flops | bytes accessed | tf_op | source)
XLA Modules:
  0.0 328.6 jit_solution(9658652034960980297)
XLA Ops:
  0.0 1.2 reduce-precision_convert_fusion
  1.2 0.0 copy-start.11
  1.2 0.2 reduce-precision_convert_fusion.1
  1.4 0.1 fusion.35
  1.5 0.3 pad_maximum_fusion.geo
  1.9 2.6 fusion.4
  4.5 0.0 copy-done.9
  4.5 0.3 reshape.175
  4.8 0.0 copy-start.6
  4.8 1.3 convolution_bitcast_fusion.2
  6.1 0.1 reshape.176
  6.2 0.0 copy-done.11
  6.2 0.1 reshape.177
  6.3 0.5 copy.73
  6.8 0.0 copy-done.6
  6.8 0.0 copy-start.10
  6.8 0.2 reshape.174.coeff
  7.1 0.0 copy-start.4
  7.1 1.6 copy-done.4
  8.7 96.0 %halo.1 = (bf16[9,64,16384]{2,1,0:T(8,128)(2,1)S(1)}, bf16[9,8,18432]{2,1,0:T(8,128)(2,1)S(1)}, bf16[9,1024,128]{2,1,0:T(8,128)(2,1)S(1)}, f32[16,8,24,128]{3,2,1,0:T(8,128)S(1)}) custom-call(bf16[64,16384]{1,0:T(8,128)(2,1)S(1)} %copy-done.4, bf16[8,18432]{1,0:T(8,128)(2,1)S(1)} %pad_maximum_fusion.geo, bf16[1024,128]{1,0:T(8,128)(2,1)S(1)} %reshape.174.coeff, ...), custom_call_target="tpu_custom_call" | custom-call | tf_op jit(solution)/shard_map/halo/pallas_call | solution.py:159
  104.7 0.0 copy-start
  104.7 6.4 %copy-done = bf16[9,64,16384]{2,1,0:T(8,128)(2,1)} copy-done((bf16[9,64,16384]{2,1,0:T(8,128)(2,1)}, bf16[9,64,16384]{2,1,0:T(8,128)(2,1)S(1)}, u32[]{:S(2)}) %copy-start) | copy-done | bytes 18874392
  111.2 1.5 copy-done.2
  112.6 1.2 copy-done.5
  113.9 0.9 slice_add_fusion
  114.8 1.3 reshape.180
  116.1 1.6 copy.35
  117.8 0.1 copy.34
  117.9 0.1 reshape.190
  118.0 6.4 %gather_fusion.1 = f32[512,3,32]{2,1,0:T(4,128)} fusion(f32[9,3,64,32]{3,1,2,0:T(4,128)} %copy.35, s32[512]{0:T(512)S(1)} %reshape.190), kind=kCustom, calls=%fused_computation.1 | custom fusion | bytes 397312 | tf_op jit(solution)/shard_map/gather | solution.py:506
  124.3 2.7 fusion.82
  127.1 0.1 copy.36
  127.2 0.1 copy.38
  127.4 0.1 copy.40
  127.5 0.0 slice-done
  127.5 0.1 squeeze.8
  127.6 0.1 copy.37
  127.7 0.1 copy.39
  127.8 0.1 copy.41
  127.9 3.5 %multiply_exponential_fusion = f32[64,8,32,32]{0,3,2,1:T(8,128)} fusion(f32[64,32]{0,1:T(8,128)S(1)} %copy.41, f32[64,8,32]{0,2,1:T(8,128)S(1)} %copy.40, f32[64,32]{0,1:T(8,128)S(1)} %copy.39, f32[64,8,32]{0,2,1:T(8,128)S(1)} %copy.38, f32[64,32]{0,1:T(8,128)S(1)} %copy.37, f32[64,8,32]{0,2,1:T(8,128)S(1)} %copy.36), kind=kLoop, calls=%fused_computation.3 | loop fusion | flops 4718592 | bytes 2318336 | tf_op jit(solution)/shard_map/exp2 | solution.py:512
  131.4 9.4 %copy.42 = f32[64,8,32,32]{2,3,1,0:T(8,128)} copy(f32[64,8,32,32]{0,3,2,1:T(8,128)} %multiply_exponential_fusion) | data formatting | bytes 4194304 | tf_op jit(solution)/shard_map/exp2 | solution.py:512
  140.7 0.0 copy-done.3
  140.7 4.1 %reshape.179 = bf16[9,32,32,2,64]{4,3,2,1,0:T(2,128)(2,1)} reshape(bf16[9,1024,128]{2,1,0:T(8,128)(2,1)S(1)} %copy-done.3) | data formatting | bytes 4718592 | tf_op jit(solution)/shard_map/reshape | solution.py:513
  144.8 5.8 %copy.33 = bf16[9,32,32,2,64]{4,2,3,1,0:T(8,128)(2,1)} copy(bf16[9,32,32,2,64]{4,3,2,1,0:T(2,128)(2,1)} %reshape.179) | data formatting | bytes 4718592 | tf_op jit(solution)/shard_map/reshape | solution.py:513
  150.7 0.1 copy.32
  150.8 0.1 reshape.184
  150.9 6.8 %gather_fusion = bf16[512,32,64]{2,1,0:T(8,128)(2,1)} fusion(bf16[9,32,32,2,64]{4,2,3,1,0:T(8,128)(2,1)} %copy.33, s32[512]{0:T(512)S(1)} %reshape.184), kind=kCustom, calls=%fused_computation | custom fusion | bytes 4200448 | tf_op jit(solution)/shard_map/gather | solution.py:514
  157.7 9.8 %convolution_bitcast_fusion.1 = f32[64,64,32]{1,2,0:T(8,128)S(1)} fusion(bf16[64,8,32,64]{3,2,1,0:T(8,128)(2,1)} %bitcast.80, f32[64,8,32,32]{2,3,1,0:T(8,128)} %copy.42), kind=kOutput, calls=%fused_computation.10 | convolution fusion | flops 402653184 | bytes 4718592 | tf_op jit(solution)/shard_map/ifsv,ifst->ivt/dot_general | solution.py:515
  167.4 0.0 copy-start.12
  167.5 0.0 copy-done.13
  167.5 2.0 gather_fusion.2
  169.5 0.1 reshape.183
  169.7 0.2 reshape.182
  169.8 0.7 fusion.17
  170.5 0.0 copy-done.7
  170.5 1.6 fusion.7
  172.1 0.0 copy-done.12
  172.1 0.1 fusion.69
  172.2 0.6 pad_add_fusion.index
  172.8 74.9 %near.1 = (bf16[9,64,64,256]{3,2,1,0:T(8,128)(2,1)}, f32[64,64,256]{2,1,0:T(8,128)}) custom-call(s32[4,384]{1,0:T(4,128)} %pad_add_fusion.index, bf16[9,64,16384]{2,1,0:T(8,128)(2,1)} %copy-done, bf16[9,8,18432]{2,1,0:T(8,128)(2,1)} %copy-done.1), custom_call_target="tpu_custom_call" | custom-call | tf_op jit(solution)/shard_map/near/pallas_call | solution.py:302
  247.7 0.0 copy-done.8
  247.7 5.0 %convolution_add_fusion.base = f32[64,64,256]{2,1,0:T(8,128)} fusion(f32[64,64,256]{2,1,0:T(8,128)} %get-tuple-element.14, bf16[64,64,32]{1,2,0:T(8,128)(2,1)S(1)} %fusion.7, bf16[4,64,8,256]{3,2,1,0:T(8,128)(2,1)S(1)} %bitcast.85), kind=kOutput, calls=%fused_computation.4 | convolution fusion | flops 68157440 | bytes 9699328 | tf_op jit(solution)/shard_map/ivr,ril->ivl/dot_general | solution.py:525
  252.6 74.0 %give_back.1 = f32[64,16384]{1,0:T(8,128)S(1)} custom-call(bf16[9,64,64,256]{3,2,1,0:T(8,128)(2,1)} %get-tuple-element.13.partial, f32[64,64,256]{2,1,0:T(8,128)} %convolution_add_fusion.base), custom_call_target="tpu_custom_call" | custom-call | tf_op jit(solution)/shard_map/give_back/pallas_call | solution.py:449
  326.6 2.0 copy.76
  (23 shorter events, 0.2 us)
Async XLA Ops:
  0.0 4.5 %copy-start.9 = (f32[32,2048]{1,0:T(8,128)S(1)}, f32[32,2048]{1,0:T(8,128)}, u32[]{:S(2)}) copy-start(f32[32,2048]{1,0:T(8,128)} %param.12) | copy-start | bytes 786436
  1.2 5.0 %copy-start.11 = (f32[3,32]{1,0:T(4,128)S(1)}, f32[3,32]{1,0:T(4,128)}, u32[]{:S(2)}) copy-start(f32[3,32]{1,0:T(4,128)} %param.14) | copy-start | bytes 1156
  4.8 2.0 copy-start.6
  6.8 110.9 %copy-start.10 = (s32[64,8]{0,1:T(8,128)S(1)}, s32[64,8]{0,1:T(8,128)}, u32[]{:S(2)}) copy-start(s32[64,8]{0,1:T(8,128)} %param.16) | copy-start | bytes 6148
  7.1 1.6 copy-start.4
  104.7 6.4 %copy-start = (bf16[9,64,16384]{2,1,0:T(8,128)(2,1)}, bf16[9,64,16384]{2,1,0:T(8,128)(2,1)S(1)}, u32[]{:S(2)}) copy-start(bf16[9,64,16384]{2,1,0:T(8,128)(2,1)S(1)} %get-tuple-element.11.vec_pool) | copy-start | bytes 56623108
  111.2 1.5 copy-start.2
  112.6 1.2 copy-start.5
  113.8 13.2 %copy-start.1 = (bf16[9,8,18432]{2,1,0:T(8,128)(2,1)}, bf16[9,8,18432]{2,1,0:T(8,128)(2,1)S(1)}, u32[]{:S(2)}) copy-start(bf16[9,8,18432]{2,1,0:T(8,128)(2,1)S(1)} %get-tuple-element.12.geo_pool) | copy-start | bytes 7962628
  117.7 9.8 %slice-start = ((f32[9,3,2048]{2,1,0:T(4,128)}), f32[1,3,2048]{2,1,0:T(4,128)S(1)}, s32[]{:S(2)}) async-start(f32[9,3,2048]{2,1,0:T(4,128)} %slice_add_fusion), calls=%async_computation | async-start | bytes 65536 | tf_op jit(solution)/shard_map/slice | solution.py:507
  131.4 9.4 %copy-start.3 = (bf16[9,1024,128]{2,1,0:T(8,128)(2,1)S(1)}, bf16[9,1024,128]{2,1,0:T(8,128)(2,1)}, u32[]{:S(2)}) copy-start(bf16[9,1024,128]{2,1,0:T(8,128)(2,1)} %copy-done.2) | copy-start | bytes 7077892
  157.7 9.8 %copy-start.13 = (s32[1,16]{1,0:T(1,128)S(1)}, s32[1,16]{1,0:T(1,128)}, u32[]{:S(2)}) copy-start(s32[1,16]{1,0:T(1,128)} %param.17) | copy-start | bytes 196
  157.7 12.8 %copy-start.7 = (f32[32,64,32]{2,1,0:T(8,128)S(1)}, f32[32,64,32]{2,1,0:T(8,128)}, u32[]{:S(2)}) copy-start(f32[32,64,32]{2,1,0:T(8,128)} %copy-done.6) | copy-start | bytes 786436
  167.4 4.7 %copy-start.12 = (s32[2,384]{1,0:T(2,128)S(1)}, s32[2,384]{1,0:T(2,128)}, u32[]{:S(2)}) copy-start(s32[2,384]{1,0:T(2,128)} %param.15) | copy-start | bytes 9220
  172.8 74.9 %copy-start.8 = (bf16[32,16384]{1,0:T(8,128)(2,1)S(1)}, bf16[32,16384]{1,0:T(8,128)(2,1)}, u32[]{:S(2)}) copy-start(bf16[32,16384]{1,0:T(8,128)(2,1)} %param.11) | copy-start | bytes 3145732

commit v2 on v1

--- a/solution.py
+++ b/solution.py
@@ -25,14 +25,6 @@
     norm = -0.5 * (whole[0:1] ** 2 + whole[1:2] ** 2 + whole[2:3] ** 2)
     norm_high = lax.reduce_precision(norm, 8, 7)
     return jnp.concatenate([high, norm_high, low, norm - norm_high], axis=0).astype(BF16)
-
-
-def kernel_block(left, right):
-    total = None
-    for dimension in range(3):
-        gap = left[..., dimension, :, None] - right[..., dimension, None, :]
-        total = gap * gap if total is None else total + gap * gap
-    return jnp.exp(-0.5 * total)
 
 
 def remote(src, dst, send, recv, device):
@@ -153,7 +145,7 @@
 def exchange(rows, cols, vec, geo, coeff, share):
     chunks = vec.shape[0] // CHUNK
     vmem = pl.BlockSpec(memory_space=pltpu.VMEM)
-    hbm = pl.BlockSpec(memory_space=pl.ANY)
+    hbm = pl.BlockSpec(memory_space=pltpu.HBM)
     pool = lambda a: jax.ShapeDtypeStruct((9, *a.shape), a.dtype)
     dma = pltpu.SemaphoreType.DMA
     return pl.pallas_call(
@@ -167,7 +159,7 @@
             dma((rows,)), dma((rows,)), dma((cols,)), dma((cols,)), dma((4,)),
         ],
         compiler_params=pltpu.CompilerParams(
-            collective_id=0, has_side_effects=True, vmem_limit_bytes=24 * 2**20
+            collective_id=0, has_side_effects=True, vmem_limit_bytes=60 * 2**20
         ),
         name="halo",
     )(vec, geo, coeff, share)
@@ -202,8 +194,6 @@
         touched[i] = 0
 
     geo_copy.wait()
-    row_id = lax.broadcasted_iota(jnp.int32, (8, width), 0)
-    unit = lax.rem(row_id, 4) == 3
 
     def features(hood, leaf):
         return feats[hood, :, pl.ds(pl.multiple_of(leaf * width, width), width)].astype(F32)
@@ -211,15 +201,7 @@
     def power(p):
         tgt = features(index[0, p], index[1, p])
         src = features(index[2, p], index[3, p])
-        turned = jnp.concatenate([tgt[4:8], tgt[0:4]], axis=0)
-        left = jnp.concatenate([src, jnp.where(unit, 1.0, src)], axis=0).astype(BF16)
-        right = jnp.concatenate(
-            [
-                jnp.where(unit, 1.0, jnp.where(row_id < 4, tgt, turned)),
-                jnp.where(row_id < 3, turned, tgt),
-            ],
-            axis=0,
-        ).astype(BF16)
+        left, right = left_rows(src).astype(BF16), right_rows(tgt).astype(BF16)
         return lax.dot_general(left, right, (((0,), (0,)), ((), ())), preferred_element_type=F32)
 
     @pl.loop(0, blocks // GROUP)
@@ -273,18 +255,10 @@
             else:
                 put(hood, part).wait()
 
-            @pl.loop(0, share)
+            @pl.loop(0, share, unroll=4)
             def _(k):
                 place = hood * leaves + part * share + k
-                slot = lax.rem(part, STAGES)
-
-                @pl.when(touched[place] > 0)
-                def _():
-                    stage[slot, k] = acc[place].astype(BF16)
-
-                @pl.when(touched[place] == 0)
-                def _():
-                    stage[slot, k] = jnp.zeros(stage.shape[2:], BF16)
+                stage[lax.rem(part, STAGES), k] = jnp.where(touched[place] > 0, acc[place], 0.0).astype(BF16)
 
             put(hood, part).start()
 
@@ -320,19 +294,89 @@
     )(index, vec_pool, geo_pool)
 
 
+def left_rows(part):
+    unit = lax.rem(lax.broadcasted_iota(jnp.int32, part.shape, 0), 4) == 3
+    return jnp.concatenate([part, jnp.where(unit, 1.0, part)], axis=0)
+
+
+def right_rows(part):
+    row_id = lax.broadcasted_iota(jnp.int32, part.shape, 0)
+    turned = jnp.concatenate([part[4:8], part[0:4]], axis=0)
+    upper = jnp.where(lax.rem(row_id, 4) == 3, 1.0, jnp.where(row_id < 4, part, turned))
+    return jnp.concatenate([upper, jnp.where(row_id < 3, turned, part)], axis=0)
+
+
+def far_field(rank, far_index, top_index, own_top, coeff, skel, skel_rows, tops, turn, field):
+    groups, vecs, lanes = field.shape
+    members = lanes // rank
+    partners = far_index.shape[1] // (groups * members)
+    first_dim = (((0,), (0,)), ((), ()))
+    lane = lax.broadcasted_iota(jnp.int32, (partners * rank, lanes), 1) // rank
+
+    @pl.loop(0, 9)
+    def _(hood):
+        @pl.loop(0, groups)
+        def _(q):
+            part = skel[hood, :, pl.ds(pl.multiple_of(q * lanes, lanes), lanes)].astype(F32)
+            turned = left_rows(part).T.astype(BF16)
+            for member in range(members):
+                skel_rows[(hood * groups + q) * members + member] = turned[member * rank : (member + 1) * rank]
+
+    top = jnp.concatenate([tops[top_index[f]] for f in range(top_index.shape[0])], axis=0)
+    total = None
+    for k in range(3):
+        gap = top[:, vecs + k : vecs + k + 1] - own_top[k : k + 1, :]
+        total = gap * gap if total is None else total + gap * gap
+    device_far = lax.dot_general(
+        top[:, :vecs], jnp.exp(-0.5 * total), first_dim, precision=HIGH, preferred_element_type=F32
+    )
+    device_far = jnp.concatenate([device_far] * members, axis=1)
+    square = lambda axis: lax.broadcasted_iota(jnp.int32, (lanes, lanes), axis) // rank
+    same = square(0) == square(1)
+
+    @pl.loop(0, groups)
+    def _(q):
+        right = right_rows(skel[4, :, pl.ds(pl.multiple_of(q * lanes, lanes), lanes)].astype(F32)).astype(BF16)
+        back = turn[:, pl.ds(pl.multiple_of(q * lanes, lanes), lanes)].T
+        back = jnp.where(same, jnp.concatenate([back] * members, axis=1), 0.0)
+        total = jnp.dot(device_far, back, precision=HIGH, preferred_element_type=F32)
+        for member in range(members):
+            lefts, coeffs = [], []
+            for f in range(partners):
+                at = (q * members + member) * partners + f
+                lefts.append(skel_rows[far_index[0, at]])
+                both = coeff[far_index[1, at]]
+                odd = jnp.full((rank, vecs), far_index[2, at], jnp.int32) > 0
+                coeffs.append(jnp.where(odd, both[:, vecs:].astype(F32), both[:, :vecs].astype(F32)))
+            left = jnp.concatenate(lefts, axis=0)
+            picked = jnp.concatenate(coeffs, axis=0).astype(BF16)
+            block = jnp.exp2(jnp.dot(left, right, preferred_element_type=F32))
+            block = jnp.where(lane == member, block, 0.0)
+            high = block.astype(BF16)
+            low = (block - high.astype(F32)).astype(BF16)
+            total += lax.dot_general(picked, high, first_dim, preferred_element_type=F32)
+            total += lax.dot_general(picked, low, first_dim, preferred_element_type=F32)
+        field[q] = total
+
+
 def return_kernel(
-    rows, cols, chunks, partial, base, out,
-    from_rows, sums, from_cols, row_send, row_recv, col_send, col_recv, local,
+    rows, cols, chunks, rank, far_index, top_index, own_top, partial, mine, coeff_pool, geo_pool, every, back, basis,
+    out,
+    from_rows, sums, from_cols, base, result, coeff, skel, skel_rows, tops, turn, base_rows, field,
+    row_send, row_recv, col_send, col_recv, local, done,
 ):
     row, col = lax.axis_index("row"), lax.axis_index("col")
     has_row = (row > 0, row < rows - 1)
     has_col = (col > 0, col < cols - 1)
     leaves, vecs, width = base.shape
     share = leaves // chunks
-    loads = [
-        pltpu.make_async_copy(partial.at[3], sums.at[0], local.at[0]),
-        pltpu.make_async_copy(partial.at[5], sums.at[1], local.at[1]),
+    points = leaves * width
+    pairs = [
+        (partial.at[3], sums.at[0]), (partial.at[5], sums.at[1]), (coeff_pool, coeff),
+        (geo_pool.at[:, :, pl.ds(points, leaves * rank)], skel), (every, tops), (back, turn),
+        (basis, base_rows), (mine, base),
     ]
+    loads = [pltpu.make_async_copy(src, dst, local.at[n]) for n, (src, dst) in enumerate(pairs)]
     for c in loads:
         c.start()
     barrier = pltpu.get_barrier_semaphore()
@@ -363,6 +407,10 @@
             col_send.at[side, c], col_recv.at[1 - side, c], col_dev[side],
         )
 
+    def put(c):
+        part = pl.ds(c * share * width, share * width)
+        return pltpu.make_async_copy(result.at[:, part], out.at[:, part], done.at[c])
+
     wanted = has_col + (True,)
     plan = [(place, c) for c in range(chunks) for place in (0, 1)] + [(2, c) for c in range(chunks)]
     for place, c in plan:
@@ -388,6 +436,7 @@
 
     for c in loads:
         c.wait()
+    far_field(rank, far_index, top_index, own_top, coeff, skel, skel_rows, tops, turn, field)
 
     for c in range(chunks):
         for place in (0, 1):
@@ -419,15 +468,24 @@
             def _(side=side, c=c):
                 col_copy(1 - side, c).wait_recv()
 
+        group = 128 // rank
+        lane = lax.broadcasted_iota(jnp.int32, (vecs, 128), 1) // rank
+
         @pl.loop(c * share, (c + 1) * share)
         def _(i):
-            out[:, pl.ds(pl.multiple_of(i * width, width), width)] = (
-                base[i]
+            points_of = pl.ds(pl.multiple_of(i * width, width), width)
+            weights = jnp.where(lane == lax.rem(i, group), field[i // group], 0.0).astype(BF16)
+            spread = jnp.concatenate([base_rows[:, points_of]] * group, axis=0)
+            result[:, points_of] = (
+                jnp.dot(weights, spread, preferred_element_type=F32)
+                + base[i]
                 + from_rows[0, 2, i].astype(F32)
                 + from_rows[1, 2, i].astype(F32)
                 + from_cols[0, i].astype(F32)
                 + from_cols[1, i].astype(F32)
             )
+
+        put(c).start()
 
     for place, c in plan:
         for side in (0, 1):
@@ -439,29 +497,42 @@
             @pl.when(has_col[side])
             def _(side=side, c=c):
                 col_copy(side, c).wait_send()
-
-
-def give_back(rows, cols, partial, base):
-    leaves, vecs, width = base.shape
+    for c in range(chunks):
+        put(c).wait()
+
+
+def give_back(rows, cols, far_index, top_index, own_top, partial, mine, coeff_pool, geo_pool, every, back, basis):
+    leaves, vecs, width = mine.shape
+    rank = basis.shape[0]
     chunks = math.gcd(leaves, 4)
-    vmem = pl.BlockSpec(memory_space=pltpu.VMEM)
+    vmem, smem = pl.BlockSpec(memory_space=pltpu.VMEM), pl.BlockSpec(memory_space=pltpu.SMEM)
+    hbm = pl.BlockSpec(memory_space=pltpu.HBM)
     dma = pltpu.SemaphoreType.DMA
     return pl.pallas_call(
-        functools.partial(return_kernel, rows, cols, chunks),
+        functools.partial(return_kernel, rows, cols, chunks, rank),
         out_shape=jax.ShapeDtypeStruct((vecs, leaves * width), F32),
-        in_specs=[pl.BlockSpec(memory_space=pl.ANY), vmem],
-        out_specs=vmem,
+        in_specs=[smem, smem, vmem] + [hbm] * 7,
+        out_specs=hbm,
         scratch_shapes=[
             pltpu.VMEM((2, 3, leaves, vecs, width), BF16),
             pltpu.VMEM((2, leaves, vecs, width), BF16),
             pltpu.VMEM((2, leaves, vecs, width), BF16),
-            dma((2, 3, chunks)), dma((2, 3, chunks)), dma((2, chunks)), dma((2, chunks)), dma((2,)),
+            pltpu.VMEM(mine.shape, F32),
+            pltpu.VMEM((vecs, leaves * width), F32),
+            pltpu.VMEM(coeff_pool.shape, BF16),
+            pltpu.VMEM((9, 8, leaves * rank), BF16),
+            pltpu.VMEM((9 * leaves, rank, 16), BF16),
+            pltpu.VMEM(every.shape, F32),
+            pltpu.VMEM(back.shape, F32),
+            pltpu.VMEM(basis.shape, BF16),
+            pltpu.VMEM((leaves * rank // 128, vecs, 128), F32),
+            dma((2, 3, chunks)), dma((2, 3, chunks)), dma((2, chunks)), dma((2, chunks)), dma((8,)), dma((chunks,)),
         ],
         compiler_params=pltpu.CompilerParams(
-            collective_id=1, has_side_effects=True, vmem_limit_bytes=48 * 2**20
+            collective_id=1, has_side_effects=True, vmem_limit_bytes=56 * 2**20
         ),
         name="give_back",
-    )(partial, base)
+    )(far_index, top_index, own_top, partial, mine, coeff_pool, geo_pool, every, back, basis)
 
 
 def shards(
@@ -487,49 +558,29 @@
         preferred_element_type=F32,
     ).astype(BF16)
     transfer_mats = transfer.reshape(rank_size, leaves, rank_size)
-    device_coeff = jnp.einsum("irv,ris->vs", coeff.astype(F32), transfer_mats, precision=HIGH)
+    device_coeff = jnp.einsum("irv,ris->sv", coeff.astype(F32), transfer_mats, precision=HIGH)
     paired = coeff.reshape(leaves // 2, 2, rank_size, vec_count)
     paired = jnp.transpose(paired, (0, 2, 1, 3)).reshape(leaves // 2 * rank_size, 2 * vec_count)
-    flat = jnp.concatenate([device_coeff.reshape(-1), device_skeleton.reshape(-1)])
-    flat = jnp.pad(flat, (0, -flat.size % 1024)).reshape(-1, 128)
-
-    vec_pool, geo_pool, coeff_pool, every = exchange(row_count, col_count, vectors, geo, paired, flat)
+    share = jnp.concatenate([device_coeff, device_skeleton.T], axis=1)
+    share = jnp.pad(share, ((0, 0), (0, 128 - share.shape[1])))
+
+    vec_pool, geo_pool, coeff_pool, every = exchange(row_count, col_count, vectors, geo, paired, share)
 
     t_hood, t_leaf = hood_of(near_pairs[0])
     s_hood, s_leaf = hood_of(near_pairs[1])
     index = jnp.stack([t_hood, t_leaf, s_hood, s_leaf])
     partial, mine = near_blocks(index, vec_pool, geo_pool, leaves, leaf_width)
 
-    far_hood, far_leaf = hood_of(far_leaves)
-    skel = geo_pool[:, :, points:].astype(F32)
-    skel = (skel[:, 0:3] + skel[:, 4:7]).reshape(9, 3, leaves, rank_size)
-    picked_skel = skel[far_hood, :, far_leaf, :]
-    own_skel = jnp.transpose(skel[4], (1, 0, 2))
-    total = None
-    for k in range(3):
-        gap = picked_skel[..., k, :, None] - own_skel[:, None, k, None, :]
-        total = gap * gap if total is None else total + gap * gap
-    coupling = jnp.exp2(-0.5 * total)
-    coeff_all = coeff_pool.reshape(9, leaves // 2, rank_size, 2, vec_count)
-    picked_coeff = coeff_all[far_hood, far_leaf // 2, :, far_leaf % 2, :].astype(F32)
-    leaf_far = jnp.einsum("ifsv,ifst->ivt", picked_coeff, coupling, precision=HIGH)
-
+    far_hood, far_leaf = hood_of(far_leaves.reshape(-1))
+    far_place = far_hood * leaves + far_leaf
+    far_index = jnp.stack([far_place, far_place // 2, far_place % 2])
     chosen = far_devices[0]
-    picked = every[chosen % col_count, chosen // col_count].reshape(chosen.shape[0], -1)
-    size = vec_count * rank_size
-    top_coeffs = picked[:, :size].reshape(-1, vec_count, rank_size)
-    top_skel = picked[:, size : size + 3 * rank_size].reshape(-1, 3, rank_size)
-    coupling_top = kernel_block(top_skel, device_skeleton[None])
-    device_far = jnp.einsum("fvs,fst->vt", top_coeffs, coupling_top, precision=HIGH)
-    field = leaf_far + jnp.einsum("vs,ris->ivr", device_far, transfer_mats, precision=HIGH)
-    far_part = jnp.einsum(
-        "ivr,ril->ivl",
-        field.astype(BF16),
-        basis.reshape(rank_size, leaves, leaf_width),
-        preferred_element_type=F32,
+    top_index = chosen % col_count * row_count + chosen // col_count
+    return give_back(
+        row_count, col_count, far_index, top_index, device_skeleton,
+        partial, mine, coeff_pool.reshape(-1, rank_size, 2 * vec_count), geo_pool,
+        every.reshape(-1, *share.shape), transfer, basis,
     )
-    base = mine + far_part
-    return give_back(row_count, col_count, partial, base)
 
 
 def solution(mesh):

time: 329 us -> 273 us (0.83)
  local copies, waits for them, and re-layouts: 55.6 us -> 6.61 us
  matrix products: 20.8 us -> 3.89 us
  Pallas kernels: 245 us -> 256 us
    dot_general x5 -> x1, matrix products: 18.2 us -> 1.3 us  [shards(): jnp.einsum('irv,ris->sv', coeff.astype(F32), transfer_mats, precision=HIGH)]
    gather x3 -> x0, local copies, waits for them, and re-layouts: 15.2 us -> none  [the longest x1 6.8 us: shards(): coeff_all[far_hood, far_leaf // 2, :, far_leaf % 2, :].astype(F32)]
    reshape x8 -> x1, local copies, waits for them, and re-layouts: 13.2 us -> 0.09 us  [shards(): far_hood, far_leaf = hood_of(far_leaves.reshape(-1))]
    pallas_call x1, Pallas kernels: 74 us -> 86.9 us  [give_back(): pl.pallas_call(functools.partial(return_kernel, rows, cols, chunks, rank)...]
    exp2 x1 -> x0, local copies, waits for them, and re-layouts: 9.37 us -> none  [shards(): coupling = jnp.exp2(-0.5 * total)]
    unnamed x30 -> x11, local copies, waits for them, and re-layouts: 12.8 us -> 4.71 us
    pallas_call x1, Pallas kernels: 74.9 us -> 70.1 us  [near_blocks(): pl.pallas_call(functools.partial(near_kernel, blocks, leaves), out_shape=...]
    exp2 x1 -> x0, other arithmetic: 3.53 us -> none  [shards(): coupling = jnp.exp2(-0.5 * total)]
where the time goes in v2:
time: 273 us
  Pallas kernels  256 us (94%)
  local copies, waits for them, and re-layouts  6.61 us (2%)
  other arithmetic  5.85 us (2%)
  matrix products  3.89 us (1%)
    pallas_call x1, Pallas kernels, exchange(): pl.pallas_call(functools.partial(halo_kernel, rows, cols), out_shape=(poo...  99.3 us
    pallas_call x1, Pallas kernels, give_back(): pl.pallas_call(functools.partial(return_kernel, rows, cols, chunks, rank)...  86.9 us
    pallas_call x1, Pallas kernels, near_blocks(): pl.pallas_call(functools.partial(near_kernel, blocks, leaves), out_shape=...  70.1 us

profile of v2, /device:TPU:35, one launch (start us, length us, event | category | flops | bytes accessed | tf_op | source)
XLA Modules:
  0.0 272.8 jit_solution(17600641697198177402)
XLA Ops:
  0.0 0.8 fusion.22
  0.8 0.6 pad_add_fusion.1.index
  1.4 1.2 reduce-precision_convert_fusion
  2.6 0.2 reduce-precision_convert_fusion.1
  2.8 0.1 fusion.12
  2.9 0.0 copy-start
  2.9 1.1 pad_maximum_fusion.geo
  4.0 2.6 fusion.3
  6.6 0.0 copy-done
  6.6 0.0 copy-start.1
  6.6 0.3 reshape.308
  6.9 1.3 convolution_bitcast_fusion
  8.2 0.0 copy-done.1
  8.2 0.1 copy.23
  8.3 0.7 select_maximum_fusion.share
  9.0 0.5 copy.42
  9.5 1.0 reshape.307.coeff
  10.5 99.3 %halo.1 = (bf16[9,64,16384]{2,1,0:T(8,128)(2,1)}, bf16[9,8,18432]{2,1,0:T(8,128)(2,1)}, bf16[9,1024,128]{2,1,0:T(8,128)(2,1)}, f32[16,8,32,128]{3,2,1,0:T(8,128)}) custom-call(bf16[64,16384]{1,0:T(8,128)(2,1)} %vec.1, bf16[8,18432]{1,0:T(8,128)(2,1)} %pad_maximum_fusion.geo, bf16[1024,128]{1,0:T(8,128)(2,1)} %reshape.307.coeff, ...), custom_call_target="tpu_custom_call" | custom-call | tf_op jit(solution)/shard_map/halo/pallas_call | solution.py:151
  109.8 0.0 copy-start.2
  109.8 0.0 copy-start.3
  109.9 70.1 %near.1 = (bf16[9,64,64,256]{3,2,1,0:T(8,128)(2,1)}, f32[64,64,256]{2,1,0:T(8,128)}) custom-call(s32[4,384]{1,0:T(4,128)} %pad_add_fusion.1.index, bf16[9,64,16384]{2,1,0:T(8,128)(2,1)} %get-tuple-element.11.vec_pool, bf16[9,8,18432]{2,1,0:T(8,128)(2,1)} %get-tuple-element.12.geo_pool), custom_call_target="tpu_custom_call" | custom-call | tf_op jit(solution)/shard_map/near/pallas_call | solution.py:276
  179.9 0.0 copy-done.2
  180.0 0.1 copy.17
  180.0 0.1 reshape.303
  180.1 0.1 and_select_fusion.1
  180.2 0.6 pad_add_fusion.far_index
  180.8 0.0 copy-done.3
  180.8 0.6 fusion.27.top_index
  181.4 86.9 %give_back.1 = f32[64,16384]{1,0:T(8,128)} custom-call(s32[3,512]{1,0:T(4,128)} %pad_add_fusion.far_index, s32[16]{0:T(128)} %fusion.27.top_index, f32[3,32]{1,0:T(4,128)} %own_top.1, bf16[9,64,64,256]{3,2,1,0:T(8,128)(2,1)} %get-tuple-element.13.partial, f32[64,64,256]{2,1,0:T(8,128)} %get-tuple-element.14.mine, bf16[288,32,128]{2,1,0:T(8,128)(2,1)} %bitcast.35, ...), custom_call_target="tpu_custom_call" | custom-call | tf_op jit(solution)/shard_map/give_back/pallas_call | solution.py:511
  268.3 4.5 %copy.44 = f32[64,16384]{1,0:T(8,128)} copy(f32[64,16384]{1,0:T(8,128)} %give_back.1) | data formatting | bytes 8388608
  (2 shorter events, 0.0 us)
Async XLA Ops:
  2.9 3.7 %copy-start = (f32[32,2048]{1,0:T(8,128)S(1)}, f32[32,2048]{1,0:T(8,128)}, u32[]{:S(2)}) copy-start(f32[32,2048]{1,0:T(8,128)} %back.1) | copy-start | bytes 786436
  6.6 1.7 copy-start.1
  109.8 70.1 %copy-start.2 = (s32[64,8]{0,1:T(8,128)S(1)}, s32[64,8]{0,1:T(8,128)}, u32[]{:S(2)}) copy-start(s32[64,8]{0,1:T(8,128)} %param.16) | copy-start | bytes 6148
  109.8 71.0 %copy-start.3 = (s32[1,16]{1,0:T(1,128)S(1)}, s32[1,16]{1,0:T(1,128)}, u32[]{:S(2)}) copy-start(s32[1,16]{1,0:T(1,128)} %param.17) | copy-start | bytes 196

commit v3 on v2

--- a/solution.py
+++ b/solution.py
@@ -36,7 +36,7 @@
 def halo_kernel(
     rows, cols, vec, geo, coeff, share,
     vec_pool, geo_pool, coeff_pool, every,
-    row_share, send, recv, row_send, row_recv, col_send, col_recv, local,
+    row_share, send, recv, turn_send, row_send, row_recv, col_send, col_recv, local,
 ):
     row, col = lax.axis_index("row"), lax.axis_index("col")
     barrier = pltpu.get_barrier_semaphore()
@@ -48,7 +48,9 @@
 
     chunks = vec.shape[0] // CHUNK
     items = chunks + 2
-    order = [0, chunks, chunks + 1] + list(range(1, chunks))
+    first = [0, chunks, chunks + 1] + list(range(1, chunks))
+    order = first[1:] + [0]
+    even = lax.rem(row, 2) == 0
 
     def own(item):
         if item < chunks:
@@ -82,23 +84,48 @@
     for k in keeps:
         k.start()
 
-    direct = [(has_right, right, 3), (has_left, left, 5), (has_down, down, 1), (has_up, up, 7)]
-    for item in order:
-        for has, device, hood in direct:
+    direct = [(has_right, right, 3, order), (has_left, left, 5, order), (has_down, down, 1, first), (has_up, up, 7, first)]
+    half = lax.rem(row, 2)
+    own_half = row_share.at[pl.ds(half * (rows // 2), rows // 2)]
+    col_copies = []
+    for n in range(items):
+        for has, device, hood, sequence in direct:
+            item = sequence[n]
+
             @pl.when(has)
             def _(device=device, hood=hood, item=item):
                 copy(own(item), hood, item, device).start()
 
-    keep_share.wait()
-    for c in row_copies:
-        c.wait_recv()
-    col_copies = []
-    for d in range(1, cols):
-        c = remote(row_share, every.at[col], col_send.at[d], col_recv.at[d], (row, lax.rem(col + d, cols)))
-        c.start()
-        col_copies.append(c)
-    keep_row = pltpu.make_async_copy(row_share, every.at[col], local.at[0])
-    keep_row.start()
+        if n == 0:
+            keep_share.wait()
+            for c in row_copies:
+                c.wait_recv()
+            for d in range(1, cols):
+                c = remote(
+                    own_half, every.at[half, col], col_send.at[d], col_recv.at[d], (row, lax.rem(col + d, cols))
+                )
+                c.start()
+                col_copies.append(c)
+            keep_row = pltpu.make_async_copy(own_half, every.at[half, col], local.at[0])
+            keep_row.start()
+
+    outward = [(1, has_up & even, 0, 2), (7, has_down & jnp.logical_not(even), 6, 8)]
+
+    def turned(hood, target, device):
+        return remote(slot(hood, 0), slot(target, 0), turn_send.at[target], recv.at[target, 0], device)
+
+    for hood, has, to_right, to_left in outward:
+        @pl.when(has)
+        def _(hood=hood, to_right=to_right, to_left=to_left):
+            copy(own(0), hood, 0, down).wait_recv()
+
+            @pl.when(has_right)
+            def _():
+                turned(hood, to_right, right).start()
+
+            @pl.when(has_left)
+            def _():
+                turned(hood, to_left, left).start()
 
     passed = [(3, has_left, 0, 6), (5, has_right, 2, 8)]
     for item in order:
@@ -107,22 +134,25 @@
             def _(hood=hood, item=item, to_down=to_down, to_up=to_up):
                 copy(own(item), hood, item, down).wait_recv()
 
-                @pl.when(has_down)
+                @pl.when(has_down & even if item == 0 else has_down)
                 def _():
                     copy(slot(hood, item), to_down, item, down).start()
 
-                @pl.when(has_up)
+                @pl.when(has_up & jnp.logical_not(even) if item == 0 else has_up)
                 def _():
                     copy(slot(hood, item), to_up, item, up).start()
 
     keep_row.wait()
+    for c in col_copies:
+        c.wait_recv()
+    swap = remote(every.at[half], every.at[half], turn_send.at[1], turn_send.at[3], (row + 1 - 2 * half, col))
+    swap.start()
     for k in keeps:
         k.wait()
-    for c in col_copies:
-        c.wait_recv()
+    odd = jnp.logical_not(even)
     for item in order:
         for has, hood in [
-            (has_up, 1), (has_down, 7),
+            (has_up & odd if item == 0 else has_up, 1), (has_down & even if item == 0 else has_down, 7),
             (has_up & has_left, 0), (has_up & has_right, 2),
             (has_down & has_left, 6), (has_down & has_right, 8),
         ]:
@@ -130,16 +160,23 @@
             def _(hood=hood, item=item):
                 copy(own(item), hood, item, down).wait_recv()
     for item in order:
+        to_down, to_up = (has_down & even, has_up & odd) if item == 0 else (has_down, has_up)
         for has, hood in [
             (has_right, 3), (has_left, 5), (has_down, 1), (has_up, 7),
-            (has_down & has_left, 0), (has_up & has_left, 6),
-            (has_down & has_right, 2), (has_up & has_right, 8),
+            (to_down & has_left, 0), (to_up & has_left, 6),
+            (to_down & has_right, 2), (to_up & has_right, 8),
         ]:
             @pl.when(has)
             def _(hood=hood, item=item):
                 copy(own(item), hood, item, down).wait_send()
+    for hood, has, to_right, to_left in outward:
+        for side, target, device in ((has_right, to_right, right), (has_left, to_left, left)):
+            @pl.when(has & side)
+            def _(hood=hood, target=target, device=device):
+                turned(hood, target, device).wait_send()
     for c in row_copies + col_copies:
         c.wait_send()
+    swap.wait()
 
 
 def exchange(rows, cols, vec, geo, coeff, share):
@@ -150,12 +187,12 @@
     dma = pltpu.SemaphoreType.DMA
     return pl.pallas_call(
         functools.partial(halo_kernel, rows, cols),
-        out_shape=(pool(vec), pool(geo), pool(coeff), jax.ShapeDtypeStruct((cols, rows, *share.shape), F32)),
+        out_shape=(pool(vec), pool(geo), pool(coeff), jax.ShapeDtypeStruct((2, cols, rows // 2, *share.shape), BF16)),
         in_specs=[vmem] * 4,
         out_specs=(hbm, hbm, hbm, vmem),
         scratch_shapes=[
-            pltpu.VMEM((rows, *share.shape), F32),
-            dma((9, chunks + 2)), dma((9, chunks + 2)),
+            pltpu.VMEM((rows, *share.shape), BF16),
+            dma((9, chunks + 2)), dma((9, chunks + 2)), dma((9,)),
             dma((rows,)), dma((rows,)), dma((cols,)), dma((cols,)), dma((4,)),
         ],
         compiler_params=pltpu.CompilerParams(
@@ -165,8 +202,9 @@
     )(vec, geo, coeff, share)
 
 
-GROUP = 8
-RING = 32
+GROUP = 32
+AHEAD = 4
+RING = 64
 STAGES = 4
 
 
@@ -210,11 +248,11 @@
         at = lax.rem(first, RING)
         for k in range(GROUP):
             fetch(first + k, at + k).wait()
-        ahead = power(first)
+        ahead = [power(first + k) for k in range(AHEAD)]
         for k in range(GROUP):
-            now = ahead
-            if k + 1 < GROUP:
-                ahead = power(first + k + 1)
+            now = ahead.pop(0)
+            if k + AHEAD < GROUP:
+                ahead.append(power(first + k + AHEAD))
             part = jnp.dot(vbuf[at + k], jnp.exp2(now).astype(BF16), preferred_element_type=F32)
             place = index[0, first + k] * leaves + index[1, first + k]
             seen = touched[place]
@@ -306,7 +344,7 @@
     return jnp.concatenate([upper, jnp.where(row_id < 3, turned, part)], axis=0)
 
 
-def far_field(rank, far_index, top_index, own_top, coeff, skel, skel_rows, tops, turn, field):
+def far_field(rank, far_index, top_index, own_top, coeff, skel, skel_rows, tops, turn, field, chunks):
     groups, vecs, lanes = field.shape
     members = lanes // rank
     partners = far_index.shape[1] // (groups * members)
@@ -322,48 +360,54 @@
             for member in range(members):
                 skel_rows[(hood * groups + q) * members + member] = turned[member * rank : (member + 1) * rank]
 
-    top = jnp.concatenate([tops[top_index[f]] for f in range(top_index.shape[0])], axis=0)
+    chosen = [tops[top_index[f]].astype(F32) for f in range(top_index.shape[0])]
+    top = jnp.concatenate([c[:rank, :vecs] + c[:rank, vecs:] for c in chosen], axis=0)
+    parts = jnp.concatenate([c[rank:].T[:rank] for c in chosen], axis=0)
+    spots = parts[:, 0:3] + parts[:, 3:6] + parts[:, 6:9]
     total = None
     for k in range(3):
-        gap = top[:, vecs + k : vecs + k + 1] - own_top[k : k + 1, :]
+        gap = spots[:, k : k + 1] - own_top[k : k + 1, :]
         total = gap * gap if total is None else total + gap * gap
     device_far = lax.dot_general(
-        top[:, :vecs], jnp.exp(-0.5 * total), first_dim, precision=HIGH, preferred_element_type=F32
+        top, jnp.exp(-0.5 * total), first_dim, precision=HIGH, preferred_element_type=F32
     )
     device_far = jnp.concatenate([device_far] * members, axis=1)
     square = lambda axis: lax.broadcasted_iota(jnp.int32, (lanes, lanes), axis) // rank
     same = square(0) == square(1)
 
-    @pl.loop(0, groups)
-    def _(q):
-        right = right_rows(skel[4, :, pl.ds(pl.multiple_of(q * lanes, lanes), lanes)].astype(F32)).astype(BF16)
-        back = turn[:, pl.ds(pl.multiple_of(q * lanes, lanes), lanes)].T
-        back = jnp.where(same, jnp.concatenate([back] * members, axis=1), 0.0)
-        total = jnp.dot(device_far, back, precision=HIGH, preferred_element_type=F32)
-        for member in range(members):
-            lefts, coeffs = [], []
-            for f in range(partners):
-                at = (q * members + member) * partners + f
-                lefts.append(skel_rows[far_index[0, at]])
-                both = coeff[far_index[1, at]]
-                odd = jnp.full((rank, vecs), far_index[2, at], jnp.int32) > 0
-                coeffs.append(jnp.where(odd, both[:, vecs:].astype(F32), both[:, :vecs].astype(F32)))
-            left = jnp.concatenate(lefts, axis=0)
-            picked = jnp.concatenate(coeffs, axis=0).astype(BF16)
-            block = jnp.exp2(jnp.dot(left, right, preferred_element_type=F32))
-            block = jnp.where(lane == member, block, 0.0)
-            high = block.astype(BF16)
-            low = (block - high.astype(F32)).astype(BF16)
-            total += lax.dot_general(picked, high, first_dim, preferred_element_type=F32)
-            total += lax.dot_general(picked, low, first_dim, preferred_element_type=F32)
-        field[q] = total
+    def part(c):
+        @pl.loop(c * groups // chunks, (c + 1) * groups // chunks)
+        def _(q):
+            right = right_rows(skel[4, :, pl.ds(pl.multiple_of(q * lanes, lanes), lanes)].astype(F32)).astype(BF16)
+            back = turn[:, pl.ds(pl.multiple_of(q * lanes, lanes), lanes)].T
+            back = jnp.where(same, jnp.concatenate([back] * members, axis=1), 0.0)
+            total = jnp.dot(device_far, back, precision=HIGH, preferred_element_type=F32)
+            for member in range(members):
+                lefts, coeffs = [], []
+                for f in range(partners):
+                    at = (q * members + member) * partners + f
+                    lefts.append(skel_rows[far_index[0, at]])
+                    both = coeff[far_index[1, at]]
+                    odd = jnp.full((rank, vecs), far_index[2, at], jnp.int32) > 0
+                    coeffs.append(jnp.where(odd, both[:, vecs:].astype(F32), both[:, :vecs].astype(F32)))
+                left = jnp.concatenate(lefts, axis=0)
+                picked = jnp.concatenate(coeffs, axis=0).astype(BF16)
+                block = jnp.exp2(jnp.dot(left, right, preferred_element_type=F32))
+                block = jnp.where(lane == member, block, 0.0)
+                high = block.astype(BF16)
+                low = (block - high.astype(F32)).astype(BF16)
+                total += lax.dot_general(picked, high, first_dim, preferred_element_type=F32)
+                total += lax.dot_general(picked, low, first_dim, preferred_element_type=F32)
+            field[q] = total
+
+    return part
 
 
 def return_kernel(
     rows, cols, chunks, rank, far_index, top_index, own_top, partial, mine, coeff_pool, geo_pool, every, back, basis,
     out,
-    from_rows, sums, from_cols, base, result, coeff, skel, skel_rows, tops, turn, base_rows, field,
-    row_send, row_recv, col_send, col_recv, local, done,
+    from_rows, sums, from_cols, base, result, coeff, skel, skel_rows, tops, turn, base_rows, field, crossed, passing,
+    row_send, row_recv, col_send, col_recv, cross_send, cross_recv, local, done,
 ):
     row, col = lax.axis_index("row"), lax.axis_index("col")
     has_row = (row > 0, row < rows - 1)
@@ -371,10 +415,16 @@
     leaves, vecs, width = base.shape
     share = leaves // chunks
     points = leaves * width
+    parity = lax.rem(row, 2)
+    leaving = (has_row[0] & (parity == 0), has_row[1] & (parity == 1))
+
+    def side_of(place):
+        return parity * 6 + place
+
     pairs = [
         (partial.at[3], sums.at[0]), (partial.at[5], sums.at[1]), (coeff_pool, coeff),
         (geo_pool.at[:, :, pl.ds(points, leaves * rank)], skel), (every, tops), (back, turn),
-        (basis, base_rows), (mine, base),
+        (basis, base_rows), (mine, base), (partial.at[side_of(1), pl.ds(0, share)], passing),
     ]
     loads = [pltpu.make_async_copy(src, dst, local.at[n]) for n, (src, dst) in enumerate(pairs)]
     for c in loads:
@@ -394,10 +444,10 @@
     def some(c):
         return pl.ds(c * share, share)
 
-    def row_copy(side, place, c):
+    def row_copy(side, place, c, src=None):
         hood = (0 if side == 0 else 6) + (0, 2, 1)[place]
         return remote(
-            partial.at[hood, some(c)], from_rows.at[1 - side, place, some(c)],
+            partial.at[hood, some(c)] if src is None else src, from_rows.at[1 - side, place, some(c)],
             row_send.at[side, place, c], row_recv.at[1 - side, place, c], row_dev[side],
         )
 
@@ -407,20 +457,39 @@
             col_send.at[side, c], col_recv.at[1 - side, c], col_dev[side],
         )
 
+    def cross_copy(side):
+        return remote(
+            partial.at[side_of(2 * side), pl.ds(0, share)], crossed.at[1 - side],
+            cross_send.at[side], cross_recv.at[1 - side], col_dev[side],
+        )
+
     def put(c):
         part = pl.ds(c * share * width, share * width)
         return pltpu.make_async_copy(result.at[:, part], out.at[:, part], done.at[c])
 
-    wanted = has_col + (True,)
-    plan = [(place, c) for c in range(chunks) for place in (0, 1)] + [(2, c) for c in range(chunks)]
+    crossing = leaving[0] | leaving[1]
+    for side in (0, 1):
+        @pl.when(crossing & has_col[side])
+        def _(side=side):
+            cross_copy(side).start()
+
+    def sent(side, place, c):
+        if c > 0:
+            return has_row[side] & (has_col[place] if place < 2 else True)
+        stays = has_row[side] & (parity != side)
+        return stays & has_col[place] if place < 2 else stays
+
+    later = list(range(1, chunks))
+    plan = [(place, 0) for place in (0, 1, 2)] + [(place, c) for c in later for place in (0, 1)]
+    plan += [(2, c) for c in later]
     for place, c in plan:
         for side in (0, 1):
-            @pl.when(has_row[side] & wanted[place])
+            @pl.when(sent(side, place, c))
             def _(side=side, place=place, c=c):
                 row_copy(side, place, c).start()
 
     def fill(ref):
-        @pl.loop(0, leaves)
+        @pl.loop(0, ref.shape[0])
         def _(i):
             ref[i] = jnp.zeros((vecs, width), BF16)
 
@@ -430,20 +499,43 @@
             for place in range(3):
                 fill(from_rows.at[side, place])
 
+        @pl.when(leaving[side])
+        def _(side=side):
+            for place in range(2):
+                fill(from_rows.at[side, place, pl.ds(0, share)])
+
         @pl.when(jnp.logical_not(has_col[side]))
         def _(side=side):
             fill(from_cols.at[side])
+            fill(crossed.at[side])
 
     for c in loads:
         c.wait()
-    far_field(rank, far_index, top_index, own_top, coeff, skel, skel_rows, tops, turn, field)
+    parts = far_field(rank, far_index, top_index, own_top, coeff, skel, skel_rows, tops, turn, field, chunks)
+
+    @pl.when(crossing)
+    def _():
+        for side in (0, 1):
+            @pl.when(has_col[side])
+            def _(side=side):
+                cross_copy(1 - side).wait_recv()
+
+        @pl.loop(0, share)
+        def _(i):
+            total = passing[i].astype(F32) + crossed[0, i].astype(F32) + crossed[1, i].astype(F32)
+            passing[i] = total.astype(BF16)
+
+        for side in (0, 1):
+            @pl.when(leaving[side])
+            def _(side=side):
+                row_copy(side, 2, 0, passing).start()
 
     for c in range(chunks):
         for place in (0, 1):
             @pl.when(has_col[place])
             def _(place=place, c=c):
                 for side in (0, 1):
-                    @pl.when(has_row[side])
+                    @pl.when(has_row[side] if c > 0 else has_row[side] & (parity != side))
                     def _(side=side):
                         row_copy(1 - side, place, c).wait_recv()
 
@@ -457,6 +549,8 @@
                     sums[place, i] = total.astype(BF16)
 
                 col_copy(place, c).start()
+
+        parts(c)
 
     for c in range(chunks):
         for side in (0, 1):
@@ -489,9 +583,17 @@
 
     for place, c in plan:
         for side in (0, 1):
-            @pl.when(has_row[side] & wanted[place])
+            @pl.when(sent(side, place, c))
             def _(side=side, place=place, c=c):
                 row_copy(side, place, c).wait_send()
+    for side in (0, 1):
+        @pl.when(leaving[side])
+        def _(side=side):
+            row_copy(side, 2, 0, passing).wait_send()
+
+        @pl.when(crossing & has_col[side])
+        def _(side=side):
+            cross_copy(side).wait_send()
     for c in range(chunks):
         for side in (0, 1):
             @pl.when(has_col[side])
@@ -522,11 +624,13 @@
             pltpu.VMEM(coeff_pool.shape, BF16),
             pltpu.VMEM((9, 8, leaves * rank), BF16),
             pltpu.VMEM((9 * leaves, rank, 16), BF16),
-            pltpu.VMEM(every.shape, F32),
+            pltpu.VMEM(every.shape, BF16),
             pltpu.VMEM(back.shape, F32),
             pltpu.VMEM(basis.shape, BF16),
             pltpu.VMEM((leaves * rank // 128, vecs, 128), F32),
-            dma((2, 3, chunks)), dma((2, 3, chunks)), dma((2, chunks)), dma((2, chunks)), dma((8,)), dma((chunks,)),
+            pltpu.VMEM((2, leaves // chunks, vecs, width), BF16),
+            pltpu.VMEM((leaves // chunks, vecs, width), BF16),
+            dma((2, 3, chunks)), dma((2, 3, chunks)), dma((2, chunks)), dma((2, chunks)), dma((2,)), dma((2,)), dma((9,)), dma((chunks,)),
         ],
         compiler_params=pltpu.CompilerParams(
             collective_id=1, has_side_effects=True, vmem_limit_bytes=56 * 2**20
@@ -561,8 +665,15 @@
     device_coeff = jnp.einsum("irv,ris->sv", coeff.astype(F32), transfer_mats, precision=HIGH)
     paired = coeff.reshape(leaves // 2, 2, rank_size, vec_count)
     paired = jnp.transpose(paired, (0, 2, 1, 3)).reshape(leaves // 2 * rank_size, 2 * vec_count)
-    share = jnp.concatenate([device_coeff, device_skeleton.T], axis=1)
-    share = jnp.pad(share, ((0, 0), (0, 128 - share.shape[1])))
+    coeff_high = lax.reduce_precision(device_coeff, 8, 7)
+    parts, rest = [], device_skeleton
+    for _ in range(3):
+        parts.append(lax.reduce_precision(rest, 8, 7))
+        rest = rest - parts[-1]
+    spots = jnp.pad(jnp.concatenate(parts, axis=0), ((0, 7), (0, 2 * vec_count - rank_size)))
+    share = jnp.concatenate(
+        [jnp.concatenate([coeff_high, device_coeff - coeff_high], axis=1), spots], axis=0
+    ).astype(BF16)
 
     vec_pool, geo_pool, coeff_pool, every = exchange(row_count, col_count, vectors, geo, paired, share)
 
@@ -575,7 +686,9 @@
     far_place = far_hood * leaves + far_leaf
     far_index = jnp.stack([far_place, far_place // 2, far_place % 2])
     chosen = far_devices[0]
-    top_index = chosen % col_count * row_count + chosen // col_count
+    rows_half = row_count // 2
+    top_row, top_col = chosen // col_count, chosen % col_count
+    top_index = (top_row // rows_half * col_count + top_col) * rows_half + top_row % rows_half
     return give_back(
         row_count, col_count, far_index, top_index, device_skeleton,
         partial, mine, coeff_pool.reshape(-1, rank_size, 2 * vec_count), geo_pool,

time: 273 us -> 219 us (0.80)
  Pallas kernels: 256 us -> 203 us
    pallas_call x1, Pallas kernels: 70.1 us -> 39.4 us  [near_blocks(): pl.pallas_call(functools.partial(near_kernel, blocks, leaves), out_shape=...]
    pallas_call x1, Pallas kernels: 86.9 us -> 75.3 us  [give_back(): pl.pallas_call(functools.partial(return_kernel, rows, cols, chunks, rank)...]
    pallas_call x1, Pallas kernels: 99.3 us -> 88.2 us  [exchange(): pl.pallas_call(functools.partial(halo_kernel, rows, cols), out_shape=(poo...]
where the time goes in v3:
time: 219 us
  Pallas kernels  203 us (93%)
  local copies, waits for them, and re-layouts  6.51 us (3%)
  other arithmetic  5.61 us (3%)
  matrix products  3.89 us (2%)
    pallas_call x1, Pallas kernels, exchange(): pl.pallas_call(functools.partial(halo_kernel, rows, cols), out_shape=(poo...  88.2 us
    pallas_call x1, Pallas kernels, give_back(): pl.pallas_call(functools.partial(return_kernel, rows, cols, chunks, rank)...  75.3 us
    pallas_call x1, Pallas kernels, near_blocks(): pl.pallas_call(functools.partial(near_kernel, blocks, leaves), out_shape=...  39.4 us
    unnamed x12, local copies, waits for them, and re-layouts  4.62 us

profile of v3, /device:TPU:35, one launch (start us, length us, event | category | flops | bytes accessed | tf_op | source)
XLA Modules:
  0.0 219.0 jit_solution(6173587670215868336)
XLA Ops:
  0.0 0.0 copy-start
  0.0 0.8 fusion.34
  0.8 0.6 pad_add_fusion.1.index
  1.4 0.7 reduce-precision_convert_fusion.4
  2.1 2.6 %fusion.3 = bf16[64,32,64]{2,1,0:T(8,128)(2,1)S(1)} fusion(bf16[8,64,8,256]{3,2,1,0:T(8,128)(2,1)} %bitcast.36, bf16[4,64,8,256]{3,2,1,0:T(8,128)(2,1)} %bitcast.39), kind=kOutput, calls=%fused_computation.3 | convolution fusion | flops 67239936 | bytes 3407872 | tf_op jit(solution)/shard_map/vil,ril->irv/dot_general | solution.py:658
  4.7 0.0 copy-done
  4.7 0.0 copy-start.1
  4.8 0.0 copy-start.2
  4.8 0.3 reshape.308
  5.1 1.3 reduce-precision_convert_fusion.2
  6.4 0.7 pad_maximum_fusion.1.share
  7.1 0.0 copy-done.1
  7.1 0.0 copy-done.2
  7.1 0.2 reduce-precision_convert_fusion
  7.3 0.2 reduce-precision_convert_fusion.1
  7.5 0.1 fusion.12
  7.6 1.1 pad_maximum_fusion.geo
  8.7 0.5 copy.42
  9.2 0.9 reshape.307.coeff
  10.1 88.2 %halo.1 = (bf16[9,64,16384]{2,1,0:T(8,128)(2,1)}, bf16[9,8,18432]{2,1,0:T(8,128)(2,1)}, bf16[9,1024,128]{2,1,0:T(8,128)(2,1)}, bf16[2,16,4,48,128]{4,3,2,1,0:T(8,128)(2,1)}) custom-call(bf16[64,16384]{1,0:T(8,128)(2,1)} %vec.1, bf16[8,18432]{1,0:T(8,128)(2,1)} %pad_maximum_fusion.geo, bf16[1024,128]{1,0:T(8,128)(2,1)} %reshape.307.coeff, ...), custom_call_target="tpu_custom_call" | custom-call | tf_op jit(solution)/shard_map/halo/pallas_call | solution.py:188
  98.3 0.0 copy-start.3
  98.3 0.0 copy-start.4
  98.3 39.4 %near.1 = (bf16[9,64,64,256]{3,2,1,0:T(8,128)(2,1)}, f32[64,64,256]{2,1,0:T(8,128)}) custom-call(s32[4,384]{1,0:T(4,128)} %pad_add_fusion.1.index, bf16[9,64,16384]{2,1,0:T(8,128)(2,1)} %get-tuple-element.11.vec_pool, bf16[9,8,18432]{2,1,0:T(8,128)(2,1)} %get-tuple-element.12.geo_pool), custom_call_target="tpu_custom_call" | custom-call | tf_op jit(solution)/shard_map/near/pallas_call | solution.py:314
  137.7 0.0 copy-done.3
  137.7 0.1 copy.16
  137.8 0.1 reshape.303
  137.9 0.1 and_select_fusion.1
  138.0 0.6 pad_add_fusion.far_index
  138.6 0.0 copy-done.4
  138.6 0.6 fusion.39.top_index
  139.2 75.3 %give_back.1 = f32[64,16384]{1,0:T(8,128)} custom-call(s32[3,512]{1,0:T(4,128)} %pad_add_fusion.far_index, s32[16]{0:T(128)} %fusion.39.top_index, f32[3,32]{1,0:T(4,128)} %own_top.1, bf16[9,64,64,256]{3,2,1,0:T(8,128)(2,1)} %get-tuple-element.13.partial, f32[64,64,256]{2,1,0:T(8,128)} %get-tuple-element.14.mine, bf16[288,32,128]{2,1,0:T(8,128)(2,1)} %bitcast.34, ...), custom_call_target="tpu_custom_call" | custom-call | tf_op jit(solution)/shard_map/give_back/pallas_call | solution.py:613
  214.5 4.5 %copy.44 = f32[64,16384]{1,0:T(8,128)} copy(f32[64,16384]{1,0:T(8,128)} %give_back.1) | data formatting | bytes 8388608
  (3 shorter events, 0.0 us)
Async XLA Ops:
  0.0 4.7 %copy-start = (f32[32,2048]{1,0:T(8,128)S(1)}, f32[32,2048]{1,0:T(8,128)}, u32[]{:S(2)}) copy-start(f32[32,2048]{1,0:T(8,128)} %back.1) | copy-start | bytes 786436
  4.7 2.4 %copy-start.1 = (f32[3,16384]{1,0:T(4,128)S(1)}, f32[3,16384]{1,0:T(4,128)}, u32[]{:S(2)}) copy-start(f32[3,16384]{1,0:T(4,128)} %param.9) | copy-start | bytes 589828
  4.8 2.4 %copy-start.2 = (f32[3,2048]{1,0:T(4,128)S(1)}, f32[3,2048]{1,0:T(4,128)}, u32[]{:S(2)}) copy-start(f32[3,2048]{1,0:T(4,128)} %param.13) | copy-start | bytes 73732
  98.3 39.4 %copy-start.3 = (s32[64,8]{0,1:T(8,128)S(1)}, s32[64,8]{0,1:T(8,128)}, u32[]{:S(2)}) copy-start(s32[64,8]{0,1:T(8,128)} %param.16) | copy-start | bytes 6148
  98.3 40.3 %copy-start.4 = (s32[1,16]{1,0:T(1,128)S(1)}, s32[1,16]{1,0:T(1,128)}, u32[]{:S(2)}) copy-start(s32[1,16]{1,0:T(1,128)} %param.17) | copy-start | bytes 196

commit v4 on v3

--- a/solution.py
+++ b/solution.py
@@ -17,14 +17,61 @@
 CHUNK = 16
 
 
+def rounded(x):
+    return x.astype(BF16).astype(F32)
+
+
 def point_features(points):
     scaled = (points - MIDDLE) * SCALE
-    high = lax.reduce_precision(scaled, 8, 7)
-    low = lax.reduce_precision(scaled - high, 8, 7)
+    high = rounded(scaled)
+    low = rounded(scaled - high)
     whole = high + low
-    norm = -0.5 * (whole[0:1] ** 2 + whole[1:2] ** 2 + whole[2:3] ** 2)
-    norm_high = lax.reduce_precision(norm, 8, 7)
+    norm = -0.5 * (whole[0:1] * whole[0:1] + whole[1:2] * whole[1:2] + whole[2:3] * whole[2:3])
+    norm_high = rounded(norm)
     return jnp.concatenate([high, norm_high, low, norm - norm_high], axis=0).astype(BF16)
+
+
+STRIP = 1024
+
+
+def own_terms(vec, coords, skeleton, basis, transfer, device_skeleton, geo, coeff, share):
+    vecs, points = vec.shape
+    rank = basis.shape[0]
+    leaves = transfer.shape[1] // rank
+    width = points // leaves
+    members = 128 // rank
+
+    def group(q, total):
+        back = transfer[:, pl.ds(pl.multiple_of(q * 128, 128), 128)].T
+        blocks = []
+        for m in range(members):
+            lanes = pl.ds(pl.multiple_of((q * members + m) * width, width), width)
+            block = lax.dot_general(
+                basis[:, lanes], vec[:, lanes], (((1,), (1,)), ((), ())), preferred_element_type=F32
+            )
+            blocks.append(rounded(block))
+        wide = jnp.concatenate([back[m * rank : (m + 1) * rank] for m in range(members)], axis=1)
+        total += jnp.dot(wide, jnp.concatenate(blocks, axis=0), precision=HIGH, preferred_element_type=F32)
+        for k in range(members // 2):
+            rows_of = pl.ds(pl.multiple_of((q * (members // 2) + k) * rank, rank), rank)
+            coeff[rows_of, :] = jnp.concatenate(blocks[2 * k : 2 * k + 2], axis=1).astype(BF16)
+        return total
+
+    device_coeff = lax.fori_loop(0, leaves // members, group, jnp.zeros((rank, vecs), F32))
+    high = rounded(device_coeff)
+    share[0:rank, :] = jnp.concatenate([high, device_coeff - high], axis=1).astype(BF16)
+    parts, rest = [], device_skeleton[...]
+    for _ in range(3):
+        parts.append(rounded(rest))
+        rest = rest - parts[-1]
+    parts.append(jnp.zeros((7, rank), F32))
+    share[rank:, :] = jnp.concatenate([jnp.concatenate(parts, axis=0)] * members, axis=1).astype(BF16)
+
+    for source, start in ((coords, 0), (skeleton, points)):
+        @pl.loop(0, source.shape[1] // STRIP)
+        def _(i, source=source, start=start):
+            at = pl.multiple_of(i * STRIP, STRIP)
+            geo[:, pl.ds(start + at, STRIP)] = point_features(source[:, pl.ds(at, STRIP)])
 
 
 def remote(src, dst, send, recv, device):
@@ -34,9 +81,9 @@
 
 
 def halo_kernel(
-    rows, cols, vec, geo, coeff, share,
+    rows, cols, vec, coords, skeleton, basis, transfer, device_skeleton,
     vec_pool, geo_pool, coeff_pool, every,
-    row_share, send, recv, turn_send, row_send, row_recv, col_send, col_recv, local,
+    geo, coeff, share, row_share, send, recv, turn_send, row_send, row_recv, col_send, col_recv, local,
 ):
     row, col = lax.axis_index("row"), lax.axis_index("col")
     barrier = pltpu.get_barrier_semaphore()
@@ -48,8 +95,8 @@
 
     chunks = vec.shape[0] // CHUNK
     items = chunks + 2
-    first = [0, chunks, chunks + 1] + list(range(1, chunks))
-    order = first[1:] + [0]
+    early = list(range(chunks))
+    order = list(range(1, chunks)) + [0, chunks, chunks + 1]
     even = lax.rem(row, 2) == 0
 
     def own(item):
@@ -68,6 +115,24 @@
     has_up, has_down = row > 0, row < rows - 1
     has_left, has_right = col > 0, col < cols - 1
     up, down, left, right = (row - 1, col), (row + 1, col), (row, col - 1), (row, col + 1)
+
+    def give(has, device, hood, item):
+        @pl.when(has)
+        def _():
+            copy(own(item), hood, item, device).start()
+
+    along_row = [(has_down, down, 1), (has_up, up, 7)]
+    along_col = [(has_right, right, 3), (has_left, left, 5)]
+    for item in early:
+        for direct in along_row:
+            give(*direct, item)
+    for item in order[:chunks]:
+        for direct in along_col:
+            give(*direct, item)
+    keeps = [pltpu.make_async_copy(vec, vec_pool.at[4], local.at[1])]
+    keeps[0].start()
+
+    own_terms(vec, coords, skeleton, basis, transfer, device_skeleton, geo, coeff, share)
 
     row_copies = []
     for d in range(1, rows):
@@ -76,38 +141,28 @@
         row_copies.append(c)
     keep_share = pltpu.make_async_copy(share, row_share.at[row], local.at[0])
     keep_share.start()
-    keeps = [
-        pltpu.make_async_copy(vec, vec_pool.at[4], local.at[1]),
-        pltpu.make_async_copy(geo, geo_pool.at[4], local.at[2]),
-        pltpu.make_async_copy(coeff, coeff_pool.at[4], local.at[3]),
-    ]
-    for k in keeps:
-        k.start()
-
-    direct = [(has_right, right, 3, order), (has_left, left, 5, order), (has_down, down, 1, first), (has_up, up, 7, first)]
+    for n, (mine, pool) in enumerate(((geo, geo_pool), (coeff, coeff_pool))):
+        keeps.append(pltpu.make_async_copy(mine, pool.at[4], local.at[2 + n]))
+        keeps[-1].start()
+    for item in (chunks, chunks + 1):
+        for direct in along_row:
+            give(*direct, item)
+
     half = lax.rem(row, 2)
     own_half = row_share.at[pl.ds(half * (rows // 2), rows // 2)]
     col_copies = []
-    for n in range(items):
-        for has, device, hood, sequence in direct:
-            item = sequence[n]
-
-            @pl.when(has)
-            def _(device=device, hood=hood, item=item):
-                copy(own(item), hood, item, device).start()
-
-        if n == 0:
-            keep_share.wait()
-            for c in row_copies:
-                c.wait_recv()
-            for d in range(1, cols):
-                c = remote(
-                    own_half, every.at[half, col], col_send.at[d], col_recv.at[d], (row, lax.rem(col + d, cols))
-                )
-                c.start()
-                col_copies.append(c)
-            keep_row = pltpu.make_async_copy(own_half, every.at[half, col], local.at[0])
-            keep_row.start()
+    keep_share.wait()
+    for c in row_copies:
+        c.wait_recv()
+    for d in range(1, cols):
+        c = remote(own_half, every.at[half, col], col_send.at[d], col_recv.at[d], (row, lax.rem(col + d, cols)))
+        c.start()
+        col_copies.append(c)
+    keep_row = pltpu.make_async_copy(own_half, every.at[half, col], local.at[0])
+    keep_row.start()
+    for item in order[chunks:]:
+        for direct in along_col:
+            give(*direct, item)
 
     outward = [(1, has_up & even, 0, 2), (7, has_down & jnp.logical_not(even), 6, 8)]
 
@@ -179,27 +234,36 @@
     swap.wait()
 
 
-def exchange(rows, cols, vec, geo, coeff, share):
+def exchange(rows, cols, vec, coords, skeleton, basis, transfer, device_skeleton):
     chunks = vec.shape[0] // CHUNK
+    rank = basis.shape[0]
     vmem = pl.BlockSpec(memory_space=pltpu.VMEM)
     hbm = pl.BlockSpec(memory_space=pltpu.HBM)
-    pool = lambda a: jax.ShapeDtypeStruct((9, *a.shape), a.dtype)
+    geo = (8, coords.shape[1] + skeleton.shape[1])
+    coeff = (transfer.shape[1] // 2, 2 * vec.shape[0])
+    share = (rank + 16, 128)
     dma = pltpu.SemaphoreType.DMA
     return pl.pallas_call(
         functools.partial(halo_kernel, rows, cols),
-        out_shape=(pool(vec), pool(geo), pool(coeff), jax.ShapeDtypeStruct((2, cols, rows // 2, *share.shape), BF16)),
-        in_specs=[vmem] * 4,
+        out_shape=(
+            jax.ShapeDtypeStruct((9, *vec.shape), BF16),
+            jax.ShapeDtypeStruct((9, *geo), BF16),
+            jax.ShapeDtypeStruct((9, *coeff), BF16),
+            jax.ShapeDtypeStruct((2, cols, rows // 2, *share), BF16),
+        ),
+        in_specs=[vmem] * 6,
         out_specs=(hbm, hbm, hbm, vmem),
         scratch_shapes=[
-            pltpu.VMEM((rows, *share.shape), BF16),
+            pltpu.VMEM(geo, BF16), pltpu.VMEM(coeff, BF16), pltpu.VMEM(share, BF16),
+            pltpu.VMEM((rows, *share), BF16),
             dma((9, chunks + 2)), dma((9, chunks + 2)), dma((9,)),
             dma((rows,)), dma((rows,)), dma((cols,)), dma((cols,)), dma((4,)),
         ],
         compiler_params=pltpu.CompilerParams(
-            collective_id=0, has_side_effects=True, vmem_limit_bytes=60 * 2**20
+            collective_id=0, has_side_effects=True, vmem_limit_bytes=58 * 2**20
         ),
         name="halo",
-    )(vec, geo, coeff, share)
+    )(vec, coords, skeleton, basis, transfer, device_skeleton)
 
 
 GROUP = 32
@@ -647,35 +711,15 @@
     rank_size, vec_count = basis.shape[0], vectors.shape[0]
     leaves = transfer.shape[1] // rank_size
     leaf_width = coords.shape[1] // leaves
-    points = coords.shape[1]
 
     def hood_of(global_leaf):
         owner = global_leaf // leaves
         hood = (owner // col_count - row_here + 1) * 3 + (owner % col_count - col_here + 1)
         return hood, global_leaf % leaves
 
-    geo = point_features(jnp.concatenate([coords, leaf_skeleton], axis=1))
-    coeff = jnp.einsum(
-        "vil,ril->irv",
-        vectors.reshape(vec_count, leaves, leaf_width),
-        basis.reshape(rank_size, leaves, leaf_width),
-        preferred_element_type=F32,
-    ).astype(BF16)
-    transfer_mats = transfer.reshape(rank_size, leaves, rank_size)
-    device_coeff = jnp.einsum("irv,ris->sv", coeff.astype(F32), transfer_mats, precision=HIGH)
-    paired = coeff.reshape(leaves // 2, 2, rank_size, vec_count)
-    paired = jnp.transpose(paired, (0, 2, 1, 3)).reshape(leaves // 2 * rank_size, 2 * vec_count)
-    coeff_high = lax.reduce_precision(device_coeff, 8, 7)
-    parts, rest = [], device_skeleton
-    for _ in range(3):
-        parts.append(lax.reduce_precision(rest, 8, 7))
-        rest = rest - parts[-1]
-    spots = jnp.pad(jnp.concatenate(parts, axis=0), ((0, 7), (0, 2 * vec_count - rank_size)))
-    share = jnp.concatenate(
-        [jnp.concatenate([coeff_high, device_coeff - coeff_high], axis=1), spots], axis=0
-    ).astype(BF16)
-
-    vec_pool, geo_pool, coeff_pool, every = exchange(row_count, col_count, vectors, geo, paired, share)
+    vec_pool, geo_pool, coeff_pool, every = exchange(
+        row_count, col_count, vectors, coords, leaf_skeleton, basis, transfer, device_skeleton
+    )
 
     t_hood, t_leaf = hood_of(near_pairs[0])
     s_hood, s_leaf = hood_of(near_pairs[1])
@@ -692,7 +736,7 @@
     return give_back(
         row_count, col_count, far_index, top_index, device_skeleton,
         partial, mine, coeff_pool.reshape(-1, rank_size, 2 * vec_count), geo_pool,
-        every.reshape(-1, *share.shape), transfer, basis,
+        every.reshape(-1, *every.shape[3:]), transfer, basis,
     )
 
 

time: 219 us -> 211 us (0.963)
  matrix products: 3.89 us -> 0 us
  other arithmetic: 5.61 us -> 2.66 us
    dot_general x2 -> x0, matrix products: 3.89 us -> none  [the longest x1 2.59 us: shards(): jnp.einsum('vil,ril->irv', vectors.reshape(vec_count, leaves, leaf_width)...]
    unnamed x12 -> x6, local copies, waits for them, and re-layouts: 4.62 us -> 4.6 us
where the time goes in v4:
time: 211 us
  Pallas kernels  203 us (96%)
  local copies, waits for them, and re-layouts  4.69 us (2%)
  other arithmetic  2.66 us (1%)
    pallas_call x1, Pallas kernels, exchange(): pl.pallas_call(functools.partial(halo_kernel, rows, cols), out_shape=(jax...  89.2 us
    pallas_call x1, Pallas kernels, give_back(): pl.pallas_call(functools.partial(return_kernel, rows, cols, chunks, rank)...  74.7 us
    pallas_call x1, Pallas kernels, near_blocks(): pl.pallas_call(functools.partial(near_kernel, blocks, leaves), out_shape=...  39.3 us
    unnamed x6, local copies, waits for them, and re-layouts  4.6 us

profile of v4, /device:TPU:35, one launch (start us, length us, event | category | flops | bytes accessed | tf_op | source)
XLA Modules:
  0.0 210.7 jit_solution(1258363744474234045)
XLA Ops:
  0.0 0.8 fusion.6
  0.8 0.6 pad_add_fusion.1.index
  1.4 89.2 %halo.1 = (bf16[9,64,16384]{2,1,0:T(8,128)(2,1)}, bf16[9,8,18432]{2,1,0:T(8,128)(2,1)}, bf16[9,1024,128]{2,1,0:T(8,128)(2,1)}, bf16[2,16,4,48,128]{4,3,2,1,0:T(8,128)(2,1)}) custom-call(bf16[64,16384]{1,0:T(8,128)(2,1)} %vec.1, f32[3,16384]{1,0:T(4,128)} %coords.1, f32[3,2048]{1,0:T(4,128)} %skeleton.1, bf16[32,16384]{1,0:T(8,128)(2,1)} %basis.3, ...), custom_call_target="tpu_custom_call" | custom-call | tf_op jit(solution)/shard_map/halo/pallas_call | solution.py:246
  90.6 0.0 copy-start
  90.6 0.0 copy-start.1
  90.6 39.3 %near.1 = (bf16[9,64,64,256]{3,2,1,0:T(8,128)(2,1)}, f32[64,64,256]{2,1,0:T(8,128)}) custom-call(s32[4,384]{1,0:T(4,128)} %pad_add_fusion.1.index, bf16[9,64,16384]{2,1,0:T(8,128)(2,1)} %get-tuple-element.11.vec_pool, bf16[9,8,18432]{2,1,0:T(8,128)(2,1)} %get-tuple-element.12.geo_pool), custom_call_target="tpu_custom_call" | custom-call | tf_op jit(solution)/shard_map/near/pallas_call | solution.py:378
  130.0 0.0 copy-done
  130.0 0.1 copy.11
  130.1 0.1 reshape.288
  130.1 0.1 and_select_fusion.1
  130.2 0.6 pad_add_fusion.far_index
  130.8 0.0 copy-done.1
  130.8 0.6 fusion.11.top_index
  131.4 74.7 %give_back.1 = f32[64,16384]{1,0:T(8,128)} custom-call(s32[3,512]{1,0:T(4,128)} %pad_add_fusion.far_index, s32[16]{0:T(128)} %fusion.11.top_index, f32[3,32]{1,0:T(4,128)} %own_top.1, bf16[9,64,64,256]{3,2,1,0:T(8,128)(2,1)} %get-tuple-element.13.partial, f32[64,64,256]{2,1,0:T(8,128)} %get-tuple-element.14.mine, bf16[288,32,128]{2,1,0:T(8,128)(2,1)} %bitcast.15, ...), custom_call_target="tpu_custom_call" | custom-call | tf_op jit(solution)/shard_map/give_back/pallas_call | solution.py:677
  206.1 4.5 %copy.13 = f32[64,16384]{1,0:T(8,128)} copy(f32[64,16384]{1,0:T(8,128)} %give_back.1) | data formatting | bytes 8388608
  (2 shorter events, 0.0 us)
Async XLA Ops:
  90.6 39.4 %copy-start = (s32[64,8]{0,1:T(8,128)S(1)}, s32[64,8]{0,1:T(8,128)}, u32[]{:S(2)}) copy-start(s32[64,8]{0,1:T(8,128)} %param.16) | copy-start | bytes 6148
  90.6 40.2 %copy-start.1 = (s32[1,16]{1,0:T(1,128)S(1)}, s32[1,16]{1,0:T(1,128)}, u32[]{:S(2)}) copy-start(s32[1,16]{1,0:T(1,128)} %param.17) | copy-start | bytes 196
